TPU v7x, 32 devices: a whole 2x2x4 slice. The times are simulated.
32 devices in a mesh: dp: 8 (over y, x, core), ctx: 4 (over z).
Axes of the slice: x: 2, y: 2, z: 4, core: 2. Of those that a mesh axis runs over, the one named last changes fastest.
Arguments:
- tokens: bfloat16 [8, 256, 768], P('dp', 'ctx'), may hold values from -6 to 6
- qkv_weight: bfloat16 [768, 2304], P(('dp', 'ctx')), may hold values from -0.21875 to 0.21875
- out_weight: bfloat16 [768, 768], P(('dp', 'ctx')), may hold values from -0.875 to 0.875
- up_weight: bfloat16 [768, 3072], P(('dp', 'ctx')), may hold values from -0.21875 to 0.21875
- down_weight: bfloat16 [3072, 768], P(('dp', 'ctx')), may hold values from -0.109375 to 0.109375
- attn_gain: bfloat16 [768], P(('dp', 'ctx')), may hold values from 0.5 to 1.5
- attn_shift: bfloat16 [768], P(('dp', 'ctx')), may hold values from -1.5 to 1.5
- ffn_gain: bfloat16 [768], P(('dp', 'ctx')), may hold values from 0.5 to 1.5
- ffn_shift: bfloat16 [768], P(('dp', 'ctx')), may hold values from -1.5 to 1.5
- pass_embed: bfloat16 [5, 768], P(None, ('dp', 'ctx')), may hold values from -3 to 3
- segment_ids: int32 [8, 256], P('dp', 'ctx'), may hold values from 0 to 3, never falling along the last dimension, each value on 1 to 128 neighbouring positions
- cotangent: bfloat16 [8, 1280, 768], P('dp', 'ctx'), may hold values from -6 to 6
Outputs:
- activations: bfloat16 [8, 1280, 768], P('dp', 'ctx')
- input_grad: float32 [8, 256, 768], P('dp', 'ctx')
- qkv_grad: float32 [768, 2304], P(('dp', 'ctx'))
- out_grad: float32 [768, 768], P(('dp', 'ctx'))
- up_grad: float32 [768, 3072], P(('dp', 'ctx'))
- down_grad: float32 [3072, 768], P(('dp', 'ctx'))
- attn_gain_grad: float32 [768], P(('dp', 'ctx'))
- attn_shift_grad: float32 [768], P(('dp', 'ctx'))
- ffn_gain_grad: float32 [768], P(('dp', 'ctx'))
- ffn_shift_grad: float32 [768], P(('dp', 'ctx'))
- pass_embed_grad: float32 [5, 768], P(None, ('dp', 'ctx'))
Inputs may be any that keep to these rules, and one draw needn't show every extreme that they name: `segment_ids`: along the positions of a sequence the document id never falls; every document spans 1 to 128 positions, and one spans exactly 128.
All inputs are finite; a program needn't handle non-finite values.
Results may differ from a plain program's by a relative error of at most 0.012.
Values may be sent and summed in bfloat16 or wider, within the bound.
A program may use at most 192 MiB of HBM per device.

v0:
```python
import jax
import jax.numpy as jnp
from jax import lax
from jax.sharding import PartitionSpec as P

H = 12


def layer_norm(entry, gain_row, shift_row):
    row_mean = jnp.mean(entry, axis=-1, keepdims=True)
    centered = entry - row_mean
    variance = jnp.mean(centered * centered, axis=-1, keepdims=True)
    return centered * lax.rsqrt(variance + 1e-05) * gain_row + shift_row


def gelu_tanh(values):
    return jax.nn.gelu(values, approximate=True)


def project(features, matrix):
    return jnp.einsum("std,de->ste", features, matrix, preferred_element_type=jnp.float32)


def project_back(features, matrix):
    return jnp.einsum("ste,de->std", features, matrix, preferred_element_type=jnp.float32)


def outer_sum(feature_list, grad_list):
    features = jnp.concatenate(feature_list, axis=1)
    grads_in = jnp.concatenate(grad_list, axis=1)
    return jnp.einsum("std,ste->de", features, grads_in, preferred_element_type=jnp.float32)


def split_heads(tensor, head_count):
    return tensor.reshape(
        tensor.shape[0], tensor.shape[1], head_count, tensor.shape[2] // head_count
    )


def merge_heads(tensor):
    return tensor.reshape(tensor.shape[0], tensor.shape[1], tensor.shape[2] * tensor.shape[3])


def stored_keys(kv_store, pass_count, model_width, head_count):
    joined = jnp.concatenate(kv_store[:pass_count], axis=1)
    return (
        split_heads(joined[:, :, :model_width], head_count),
        split_heads(joined[:, :, model_width:], head_count),
    )


def score_block(queries, key_heads, allowed_now):
    scores = (
        jnp.einsum("sqhe,skhe->shqk", queries, key_heads, preferred_element_type=jnp.float32)
        * 0.125
    )
    return jnp.where(allowed_now[:, None], scores, -1e30)


def on_device(
    tokens,
    qkv_weight,
    out_weight,
    up_weight,
    down_weight,
    attn_gain,
    attn_shift,
    ffn_gain,
    ffn_shift,
    pass_embed,
    segment_ids,
    cotangent,
):
    seq_count, local_tok, model_width = tokens.shape
    repeats = pass_embed.shape[0]
    head_count = H
    full_tok = local_tok * lax.axis_size("ctx")
    all_ids = lax.all_gather(segment_ids, "ctx", axis=1, tiled=True)
    query_pos = lax.axis_index("ctx") * local_tok + jnp.arange(local_tok, dtype=jnp.int32)
    key_pos = jnp.arange(full_tok, dtype=jnp.int32)
    allowed = (segment_ids[:, :, None] == all_ids[:, None, :]) & (
        key_pos[None, None, :] <= query_pos[None, :, None]
    )
    current = tokens.astype(jnp.float32)
    log_totals = []
    kv_store = []
    pass_outputs = []
    normed_keep = []
    query_keep = []
    attended_keep = []
    normed_mid_keep = []
    activated_keep = []
    first_backs = []
    second_backs = []
    gelu_backs = []
    for repeat in range(repeats):
        params = (
            lax.all_gather(qkv_weight, ("dp", "ctx"), axis=0, tiled=True),
            lax.all_gather(out_weight, ("dp", "ctx"), axis=0, tiled=True),
            lax.all_gather(up_weight, ("dp", "ctx"), axis=0, tiled=True),
            lax.all_gather(down_weight, ("dp", "ctx"), axis=0, tiled=True),
            lax.all_gather(attn_gain, ("dp", "ctx"), axis=0, tiled=True),
            lax.all_gather(attn_shift, ("dp", "ctx"), axis=0, tiled=True),
            lax.all_gather(ffn_gain, ("dp", "ctx"), axis=0, tiled=True),
            lax.all_gather(ffn_shift, ("dp", "ctx"), axis=0, tiled=True),
            lax.all_gather(pass_embed, ("dp", "ctx"), axis=1, tiled=True),
        )
        (
            qkv_full,
            out_full,
            up_full,
            down_full,
            gain_first,
            shift_first,
            gain_second,
            shift_second,
            embed_full,
        ) = params
        entry = current + embed_full[repeat].astype(jnp.float32)
        normed, norm_first_back = jax.vjp(
            layer_norm, entry, gain_first.astype(jnp.float32), shift_first.astype(jnp.float32)
        )
        normed_lo = normed.astype(jnp.bfloat16)
        projected = project(normed_lo, qkv_full).astype(jnp.bfloat16)
        local_kv = projected[:, :, model_width:]
        kv_store.append(lax.all_gather(local_kv, "ctx", axis=1, tiled=True))
        key_heads, value_heads = stored_keys(kv_store, repeat + 1, model_width, head_count)
        queries = split_heads(projected[:, :, :model_width], head_count)
        allowed_now = jnp.tile(allowed, (1, 1, repeat + 1))
        scores = score_block(queries, key_heads, allowed_now)
        row_max = jnp.max(scores, axis=-1, keepdims=True)
        shifted = jnp.exp(scores - row_max)
        total_exp = jnp.sum(shifted, axis=-1, keepdims=True)
        log_totals.append(row_max + jnp.log(total_exp))
        probs_lo = (shifted / total_exp).astype(jnp.bfloat16)
        attended = merge_heads(
            jnp.einsum("shqk,skhe->sqhe", probs_lo, value_heads, preferred_element_type=jnp.float32)
        ).astype(jnp.bfloat16)
        middle = entry + project(attended, out_full)
        normed_mid, norm_second_back = jax.vjp(
            layer_norm, middle, gain_second.astype(jnp.float32), shift_second.astype(jnp.float32)
        )
        normed_mid_lo = normed_mid.astype(jnp.bfloat16)
        activated, gelu_back = jax.vjp(gelu_tanh, project(normed_mid_lo, up_full))
        activated_lo = activated.astype(jnp.bfloat16)
        current = middle + project(activated_lo, down_full)
        pass_outputs.append(current.astype(jnp.bfloat16))
        normed_keep.append(normed_lo)
        query_keep.append(queries)
        attended_keep.append(attended)
        normed_mid_keep.append(normed_mid_lo)
        activated_keep.append(activated_lo)
        first_backs.append(norm_first_back)
        second_backs.append(norm_second_back)
        gelu_backs.append(gelu_back)
    small_totals = [jnp.zeros((model_width,), jnp.float32) for slot in range(4)]
    key_grads = [
        jnp.zeros((seq_count, full_tok, 2 * model_width), jnp.float32) for earlier in range(repeats)
    ]
    branch_keep = [None] * repeats
    hidden_keep = [None] * repeats
    attn_out_keep = [None] * repeats
    proj_keep = [None] * repeats
    embed_rows = [None] * repeats
    carry = jnp.zeros((seq_count, local_tok, model_width), jnp.float32)
    cot_split = cotangent.reshape(seq_count, local_tok, repeats, model_width)
    for repeat in reversed(range(repeats)):
        params = (
            lax.all_gather(qkv_weight, ("dp", "ctx"), axis=0, tiled=True),
            lax.all_gather(out_weight, ("dp", "ctx"), axis=0, tiled=True),
            lax.all_gather(up_weight, ("dp", "ctx"), axis=0, tiled=True),
            lax.all_gather(down_weight, ("dp", "ctx"), axis=0, tiled=True),
            lax.all_gather(attn_gain, ("dp", "ctx"), axis=0, tiled=True),
            lax.all_gather(attn_shift, ("dp", "ctx"), axis=0, tiled=True),
            lax.all_gather(ffn_gain, ("dp", "ctx"), axis=0, tiled=True),
            lax.all_gather(ffn_shift, ("dp", "ctx"), axis=0, tiled=True),
            lax.all_gather(pass_embed, ("dp", "ctx"), axis=1, tiled=True),
        )
        (
            qkv_full,
            out_full,
            up_full,
            down_full,
            gain_first,
            shift_first,
            gain_second,
            shift_second,
            embed_full,
        ) = params
        grad_out = cot_split[:, :, repeat].astype(jnp.float32) + carry
        queries = query_keep[repeat]
        key_heads, value_heads = stored_keys(kv_store, repeat + 1, model_width, head_count)
        allowed_now = jnp.tile(allowed, (1, 1, repeat + 1))
        attn_probs = jnp.exp(score_block(queries, key_heads, allowed_now) - log_totals[repeat])
        probs_lo = attn_probs.astype(jnp.bfloat16)
        branch_grad = grad_out.astype(jnp.bfloat16)
        branch_keep[repeat] = branch_grad
        hidden_grad = gelu_backs[repeat](project_back(branch_grad, down_full))[0].astype(
            jnp.bfloat16
        )
        hidden_keep[repeat] = hidden_grad
        middle_grad, gain_second_grad, shift_second_grad = second_backs[repeat](
            project_back(hidden_grad, up_full)
        )
        small_totals[2] = small_totals[2] + gain_second_grad
        small_totals[3] = small_totals[3] + shift_second_grad
        middle_grad = middle_grad + grad_out
        attn_out_grad = middle_grad.astype(jnp.bfloat16)
        attn_out_keep[repeat] = attn_out_grad
        mixed_grad = split_heads(
            project_back(attn_out_grad, out_full).astype(jnp.bfloat16), head_count
        )
        prob_grad = jnp.einsum(
            "sqhe,skhe->shqk", mixed_grad, value_heads, preferred_element_type=jnp.float32
        )
        score_grad = (
            attn_probs * (prob_grad - jnp.sum(prob_grad * attn_probs, axis=-1, keepdims=True))
        ).astype(jnp.bfloat16)
        query_grad = (
            jnp.einsum("shqk,skhe->sqhe", score_grad, key_heads, preferred_element_type=jnp.float32)
            * 0.125
        )
        key_grad = (
            jnp.einsum("shqk,sqhe->skhe", score_grad, queries, preferred_element_type=jnp.float32)
            * 0.125
        )
        value_grad = jnp.einsum(
            "shqk,sqhe->skhe", probs_lo, mixed_grad, preferred_element_type=jnp.float32
        )
        joined_grad = jnp.concatenate([merge_heads(key_grad), merge_heads(value_grad)], axis=-1)
        for earlier in range(repeat + 1):
            key_grads[earlier] = (
                key_grads[earlier] + joined_grad[:, earlier * full_tok : (earlier + 1) * full_tok]
            )
        pass_grads = key_grads[repeat]
        own_grad = lax.psum_scatter(
            pass_grads.astype(jnp.bfloat16), "ctx", scatter_dimension=1, tiled=True
        ).astype(jnp.float32)
        proj_grad = jnp.concatenate([merge_heads(query_grad), own_grad], axis=-1).astype(
            jnp.bfloat16
        )
        proj_keep[repeat] = proj_grad
        entry_grad, gain_first_grad, shift_first_grad = first_backs[repeat](
            project_back(proj_grad, qkv_full)
        )
        small_totals[0] = small_totals[0] + gain_first_grad
        small_totals[1] = small_totals[1] + shift_first_grad
        carry = entry_grad + middle_grad
        embed_rows[repeat] = jnp.sum(carry, axis=(0, 1))
    qkv_total = outer_sum(normed_keep, proj_keep)
    out_total = outer_sum(attended_keep, attn_out_keep)
    up_total = outer_sum(normed_mid_keep, hidden_keep)
    down_total = outer_sum(activated_keep, branch_keep)
    embed_grad = jnp.stack(embed_rows, axis=0)
    reduced = (
        lax.psum_scatter(qkv_total, ("dp", "ctx"), scatter_dimension=0, tiled=True),
        lax.psum_scatter(out_total, ("dp", "ctx"), scatter_dimension=0, tiled=True),
        lax.psum_scatter(up_total, ("dp", "ctx"), scatter_dimension=0, tiled=True),
        lax.psum_scatter(down_total, ("dp", "ctx"), scatter_dimension=0, tiled=True),
        lax.psum_scatter(small_totals[0], ("dp", "ctx"), scatter_dimension=0, tiled=True),
        lax.psum_scatter(small_totals[1], ("dp", "ctx"), scatter_dimension=0, tiled=True),
        lax.psum_scatter(small_totals[2], ("dp", "ctx"), scatter_dimension=0, tiled=True),
        lax.psum_scatter(small_totals[3], ("dp", "ctx"), scatter_dimension=0, tiled=True),
        lax.psum_scatter(embed_grad, ("dp", "ctx"), scatter_dimension=1, tiled=True),
    )
    activations = jnp.stack(pass_outputs, axis=2).reshape(
        seq_count, local_tok * repeats, model_width
    )
    return (
        activations,
        carry,
        reduced[0],
        reduced[1],
        reduced[2],
        reduced[3],
        reduced[4],
        reduced[5],
        reduced[6],
        reduced[7],
        reduced[8],
    )


def solution(mesh):
    return jax.shard_map(
        on_device,
        mesh=mesh,
        in_specs=(
            P("dp", "ctx", None),
            P(("dp", "ctx"), None),
            P(("dp", "ctx"), None),
            P(("dp", "ctx"), None),
            P(("dp", "ctx"), None),
            P(("dp", "ctx")),
            P(("dp", "ctx")),
            P(("dp", "ctx")),
            P(("dp", "ctx")),
            P(None, ("dp", "ctx")),
            P("dp", "ctx"),
            P("dp", "ctx", None),
        ),
        out_specs=(
            P("dp", "ctx", None),
            P("dp", "ctx", None),
            P(("dp", "ctx"), None),
            P(("dp", "ctx"), None),
            P(("dp", "ctx"), None),
            P(("dp", "ctx"), None),
            P(("dp", "ctx")),
            P(("dp", "ctx")),
            P(("dp", "ctx")),
            P(("dp", "ctx")),
            P(None, ("dp", "ctx")),
        ),
        check_vma=False,
    )
```

profile of v0, /device:TPU:0, one launch (start us, length us, event | category | flops | bytes accessed | tf_op | source)
XLA Modules:
  0.0 1222.9 jit_solution(17202442644714355164)
XLA Ops:
  14.6 42.3 %all-reduce.11 = (bf16[768]{0:T(1024)(128)(2,1)S(1)}, bf16[768]{0:T(1024)(128)(2,1)S(1)}, bf16[768]{0:T(1024)(128)(2,1)S(1)}, bf16[768]{0:T(1024)(128)(2,1)S(1)}) all-reduce(bf16[768]{0:T(1024)(128)(2,1)S(1)} %dynamic-update-slice.1, bf16[768]{0:T(1024)(128)(2,1)S(1)} %dynamic-update-slice, ...), channel_id=1, replica_groups=mesh['dp'=8,'ctx'=4] {'dp','ctx'}, use_global_device_ids=true, to_apply=%add.1 | all-reduce | flops 3072 | bytes 12288
  58.4 8.2 all-reduce.2
  69.4 64.6 %all-gather = bf16[32,24,5]{1,2,0:T(8,128)(2,1)S(1)} all-gather(bf16[1,24,5]{1,2,0:T(8,128)(2,1)} %bitcast.780), channel_id=1, replica_groups=mesh['dp'=8,'ctx'=4] {'dp','ctx'}, dimensions={0}, use_global_device_ids=true | all-gather | bytes 7920 | tf_op jit(solution)/shard_map/all_gather | solution.py:106
  138.8 2.8 fusion.2
  141.9 19.1 %all_gather.36 = bf16[1,256,1536]{2,1,0:T(8,128)(2,1)S(1)} all-gather(bf16[1,64,1536]{2,1,0:T(8,128)(2,1)S(1)} %slice.188), channel_id=1, replica_groups=mesh['dp'=8,'ctx'=4] {'ctx'}, dimensions={1}, use_global_device_ids=true | all-gather | bytes 983040 | tf_op jit(solution)/shard_map/all_gather | solution.py:126
  167.3 28.8 %all-gather.10.cloned.1.call-done = bf16[768,3072]{1,0:T(8,128)(2,1)} async-done(((bf16[24,3072]{1,0:T(8,128)(2,1)}), bf16[768,3072]{1,0:T(8,128)(2,1)}) %all-gather.10.cloned.1.call-update) | async-done | bytes 4718608 | tf_op jit(solution)/shard_map/all_gather | solution.py:100
  196.1 4.5 bitcast_dynamic-update-slice_fusion.4
  200.6 60.1 %all-gather.12.cloned.1.call-done = bf16[3072,768]{1,0:T(8,128)(2,1)} async-done(((bf16[96,768]{1,0:T(8,128)(2,1)}), bf16[3072,768]{1,0:T(8,128)(2,1)}) %all-gather.12.cloned.1.call-update) | async-done | bytes 4718608 | tf_op jit(solution)/shard_map/all_gather | solution.py:101
  260.7 4.4 constant_dynamic-update-slice_fusion.17
  269.6 18.4 %all_gather.44 = bf16[1,256,1536]{2,1,0:T(8,128)(2,1)S(1)} all-gather(bf16[1,64,1536]{2,1,0:T(8,128)(2,1)} %slice.193), channel_id=1, replica_groups=mesh['dp'=8,'ctx'=4] {'ctx'}, dimensions={1}, use_global_device_ids=true | all-gather | bytes 983040 | tf_op jit(solution)/shard_map/all_gather | solution.py:126
  310.4 18.2 %all_gather.45 = bf16[1,256,1536]{2,1,0:T(8,128)(2,1)S(1)} all-gather(bf16[1,64,1536]{2,1,0:T(8,128)(2,1)} %slice.198), channel_id=1, replica_groups=mesh['dp'=8,'ctx'=4] {'ctx'}, dimensions={1}, use_global_device_ids=true | all-gather | bytes 983040 | tf_op jit(solution)/shard_map/all_gather | solution.py:126
  330.2 3.2 fusion.259
  353.3 29.3 %all_gather.46 = bf16[1,256,1536]{2,1,0:T(8,128)(2,1)S(1)} all-gather(bf16[1,64,1536]{2,1,0:T(8,128)(2,1)} %slice.203), channel_id=1, replica_groups=mesh['dp'=8,'ctx'=4] {'ctx'}, dimensions={1}, use_global_device_ids=true | all-gather | bytes 983040 | tf_op jit(solution)/shard_map/all_gather | solution.py:126
  383.9 3.7 fusion.258
  405.9 17.0 %all_gather.47 = bf16[1,256,1536]{2,1,0:T(8,128)(2,1)S(1)} all-gather(bf16[1,64,1536]{2,1,0:T(8,128)(2,1)S(1)} %slice.208), channel_id=1, replica_groups=mesh['dp'=8,'ctx'=4] {'ctx'}, dimensions={1}, use_global_device_ids=true | all-gather | bytes 983040 | tf_op jit(solution)/shard_map/all_gather | solution.py:126
  423.8 4.4 fusion.257
  430.9 4.6 copy.113
  450.6 4.0 multiply_reduce_fusion
  461.0 3.6 copy.137
  466.0 2.9 fusion.63
  468.9 19.5 %reduce-scatter.29.cloned.1.call-done = bf16[64,1536]{1,0:T(8,128)(2,1)} async-done(((bf16[256,1536]{1,0:T(8,128)(2,1)}), bf16[64,1536]{1,0:T(8,128)(2,1)}) %reduce-scatter.29.cloned.1.call-update) | async-done | bytes 196624
  490.0 4.0 fusion.157
  495.0 4.0 fusion.106
  503.7 3.0 multiply_reduce_fusion.1
  514.8 4.9 copy.139
  525.5 19.5 %reduce-scatter.31.cloned.1.call-done = bf16[64,1536]{1,0:T(8,128)(2,1)} async-done(((bf16[256,1536]{1,0:T(8,128)(2,1)}), bf16[64,1536]{1,0:T(8,128)(2,1)}) %reduce-scatter.31.cloned.1.call-update) | async-done | bytes 196624
  546.7 4.1 fusion.156
  552.4 4.0 fusion.99
  571.4 4.8 copy.141
  580.7 20.8 %reduce-scatter.33.cloned.1.call-done = bf16[64,1536]{1,0:T(8,128)(2,1)} async-done(((bf16[256,1536]{1,0:T(8,128)(2,1)}), bf16[64,1536]{1,0:T(8,128)(2,1)}) %reduce-scatter.33.cloned.1.call-update) | async-done | bytes 196624
  603.2 4.0 fusion.155
  608.2 4.0 fusion.92
  625.8 3.0 copy.143
  633.8 20.3 %reduce-scatter.35.cloned.1.call-done = bf16[64,1536]{1,0:T(8,128)(2,1)} async-done(((bf16[256,1536]{1,0:T(8,128)(2,1)}), bf16[64,1536]{1,0:T(8,128)(2,1)}) %reduce-scatter.35.cloned.1.call-update) | async-done | bytes 196624
  655.9 4.1 fusion.154
  661.6 4.7 bitcast_dynamic-update-slice_fusion.9
  674.8 2.9 fusion.46
  690.0 13.1 %reduce-scatter.37.cloned.1.call-done = bf16[64,1536]{1,0:T(8,128)(2,1)} async-done(((bf16[256,1536]{1,0:T(8,128)(2,1)}), bf16[64,1536]{1,0:T(8,128)(2,1)}) %reduce-scatter.37.cloned.1.call-update) | async-done | bytes 196624
  706.0 4.5 concatenate.200
  710.5 6.0 fusion.20
  719.7 5.2 fusion.15
  726.8 5.0 fusion.13
  733.4 4.0 fusion.78
  760.5 3.6 fusion.158
  770.4 39.5 %all-reduce.10 = (f32[768]{0:T(1024)S(1)}, f32[768]{0:T(1024)S(1)}, f32[768]{0:T(1024)S(1)}, f32[768]{0:T(1024)S(1)}, f32[5,768]{1,0:T(8,128)S(1)}) all-reduce(f32[768]{0:T(1024)S(1)} %get-tuple-element.173, f32[768]{0:T(1024)S(1)} %get-tuple-element.172, ...), channel_id=11, replica_groups=mesh['dp'=8,'ctx'=4] {'dp','ctx'}, use_global_device_ids=true, to_apply=%region_69.70.clone | all-reduce | flops 6912 | bytes 55296
  813.0 119.9 %reduce-scatter.21.cloned.1.call-done = f32[24,2304]{1,0:T(8,128)} async-done(((f32[768,2304]{1,0:T(8,128)}), f32[24,2304]{1,0:T(8,128)}) %reduce-scatter.21.cloned.1.call-update) | async-done | bytes 221200 | tf_op jit(solution)/shard_map/reduce_scatter | solution.py:256
  932.9 141.6 %reduce-scatter.25.cloned.1.call-done = f32[24,3072]{1,0:T(8,128)} async-done(((f32[768,3072]{1,0:T(8,128)}), f32[24,3072]{1,0:T(8,128)}) %reduce-scatter.25.cloned.1.call-update) | async-done | bytes 294928 | tf_op jit(solution)/shard_map/reduce_scatter | solution.py:258
  1074.4 141.6 %reduce-scatter.27.cloned.1.call-done = f32[96,768]{1,0:T(8,128)} async-done(((f32[3072,768]{1,0:T(8,128)}), f32[96,768]{1,0:T(8,128)}) %reduce-scatter.27.cloned.1.call-update) | async-done | bytes 294928 | tf_op jit(solution)/shard_map/reduce_scatter | solution.py:259
  (897 shorter events, 244.3 us)
Async XLA Ops:
  7.2 129.6 %copy-start.71 = (bf16[1,64,768]{2,1,0:T(8,128)(2,1)S(1)}, bf16[1,64,768]{2,1,0:T(8,128)(2,1)}, u32[]{:S(2)}) copy-start(bf16[1,64,768]{2,1,0:T(8,128)(2,1)} %param.12) | copy-start | bytes 294916
  7.2 131.6 %all-gather.6.cloned.1.call-start = ((), (), s32[]{:S(2)}) async-start(), calls=%async_computation.9 | async-start | bytes 3649536 | tf_op jit(solution)/shard_map/all_gather | solution.py:98
  7.9 155.3 %all-gather.8.cloned.1.call-start = ((), (), s32[]{:S(2)}) async-start(), calls=%async_computation.10 | async-start | bytes 1216512 | tf_op jit(solution)/shard_map/all_gather | solution.py:99
  8.7 187.5 %all-gather.10.cloned.1.call-start = ((), (), s32[]{:S(2)}) async-start(), calls=%async_computation.11 | async-start | bytes 4866048 | tf_op jit(solution)/shard_map/all_gather | solution.py:100
  9.4 251.3 %all-gather.12.cloned.1.call-start = ((), (), s32[]{:S(2)}) async-start(), calls=%async_computation.12 | async-start | bytes 4866048 | tf_op jit(solution)/shard_map/all_gather | solution.py:101
  10.0 478.3 %reduce-scatter.29.cloned.1.call-start = ((), (), s32[]{:S(2)}) async-start(), calls=%async_computation.17 | async-start | bytes 983040
  136.8 26.5 %copy-start.161 = (f32[768]{0:T(1024)}, f32[768]{0:T(1024)S(1)}, u32[]{:S(2)}) copy-start(f32[768]{0:T(1024)S(1)} %get-tuple-element.35) | copy-start | bytes 9220
  141.9 20.0 %copy-start.130 = (bf16[1,64,768]{1,2,0:T(8,128)(2,1)}, bf16[1,64,768]{1,2,0:T(8,128)(2,1)S(1)}, u32[]{:S(2)}) copy-start(bf16[1,64,768]{1,2,0:T(8,128)(2,1)S(1)} %copy.159) | copy-start | bytes 294916
  165.1 35.5 %copy-start.51 = (f32[1,64,768]{2,1,0:T(8,128)}, f32[1,64,768]{2,1,0:T(8,128)S(1)}, u32[]{:S(2)}) copy-start(f32[1,64,768]{2,1,0:T(8,128)S(1)} %get-tuple-element.108) | copy-start | bytes 589828
  165.1 35.5 %copy-start.197 = (f32[64]{0:T(128)}, f32[64]{0:T(128)S(1)}, u32[]{:S(2)}) copy-start(f32[64]{0:T(128)S(1)} %broadcast_multiply_fusion.8) | copy-start | bytes 772
  165.3 35.3 %copy-start.245 = (f32[64]{0:T(128)}, f32[64]{0:T(128)S(1)}, u32[]{:S(2)}) copy-start(f32[64]{0:T(128)S(1)} %multiply_reduce_fusion.13) | copy-start | bytes 772
  165.3 35.3 %copy-start.218 = (f32[64]{0:T(128)}, f32[64]{0:T(128)S(1)}, u32[]{:S(2)}) copy-start(f32[64]{0:T(128)S(1)} %fusion.227) | copy-start | bytes 772
  465.7 79.3 %reduce-scatter.31.cloned.1.call-start = ((), (), s32[]{:S(2)}) async-start(), calls=%async_computation.18 | async-start | bytes 983040
  466.0 24.0 %copy-start.216 = (f32[64]{0:T(128)S(1)}, f32[64]{0:T(128)}, u32[]{:S(2)}) copy-start(f32[64]{0:T(128)} %copy-done.215) | copy-start | bytes 772
  466.0 24.0 %copy-start.242 = (f32[64]{0:T(128)S(1)}, f32[64]{0:T(128)}, u32[]{:S(2)}) copy-start(f32[64]{0:T(128)} %copy-done.241) | copy-start | bytes 772
  466.0 28.3 %copy-start.108 = (bf16[1,64,1,768]{3,2,1,0:T(2,128)(2,1)S(1)}, bf16[1,64,1,768]{3,2,1,0:T(2,128)(2,1)}, u32[]{:S(2)}) copy-start(bf16[1,64,1,768]{3,2,1,0:T(2,128)(2,1)} %get-tuple-element.89) | copy-start | bytes 294916
  466.0 33.8 %slice-start.8 = ((s8[4718592]{0:T(1024)(128)(4,1)}), s8[524288]{0:T(1024)(128)(4,1)S(1)}, s32[]{:S(2)}) async-start(s8[4718592]{0:T(1024)(128)(4,1)} %bitcast.650), calls=%async_computation.30 | async-start | bytes 1048576
  468.9 25.1 %copy-start.147 = (bf16[12,64,64]{2,1,0:T(8,128)(2,1)}, bf16[12,64,64]{2,1,0:T(8,128)(2,1)S(1)}, u32[]{:S(2)}) copy-start(bf16[12,64,64]{2,1,0:T(8,128)(2,1)S(1)} %fusion.63) | copy-start | bytes 294916
  522.2 79.3 %reduce-scatter.33.cloned.1.call-start = ((), (), s32[]{:S(2)}) async-start(), calls=%async_computation.19 | async-start | bytes 983040
  522.7 23.9 %copy-start.46 = (f32[1,64,768]{2,1,0:T(8,128)S(1)}, f32[1,64,768]{2,1,0:T(8,128)}, u32[]{:S(2)}) copy-start(f32[1,64,768]{2,1,0:T(8,128)} %copy-done.44) | copy-start | bytes 589828
  522.7 23.9 %copy-start.169 = (f32[768]{0:T(1024)S(1)}, f32[768]{0:T(1024)}, u32[]{:S(2)}) copy-start(f32[768]{0:T(1024)} %get-tuple-element.32) | copy-start | bytes 9220
  522.7 23.9 %copy-start.213 = (f32[64]{0:T(128)S(1)}, f32[64]{0:T(128)}, u32[]{:S(2)}) copy-start(f32[64]{0:T(128)} %copy-done.212) | copy-start | bytes 772
  522.7 23.9 %copy-start.239 = (f32[64]{0:T(128)S(1)}, f32[64]{0:T(128)}, u32[]{:S(2)}) copy-start(f32[64]{0:T(128)} %copy-done.238) | copy-start | bytes 772
  522.7 34.4 %slice-start.10 = ((s8[4718592]{0:T(1024)(128)(4,1)}), s8[524288]{0:T(1024)(128)(4,1)S(1)}, s32[]{:S(2)}) async-start(s8[4718592]{0:T(1024)(128)(4,1)} %bitcast.652), calls=%async_computation.32 | async-start | bytes 1048576
  560.1 47.3 %copy-start.101 = (f32[1,64,768]{2,1,0:T(8,128)}, f32[1,64,768]{2,1,0:T(8,128)S(1)}, u32[]{:S(2)}) copy-start(f32[1,64,768]{2,1,0:T(8,128)S(1)} %add_add_fusion.15) | copy-start | bytes 589828
  578.6 24.5 %copy-start.43 = (f32[1,64,768]{2,1,0:T(8,128)S(1)}, f32[1,64,768]{2,1,0:T(8,128)}, u32[]{:S(2)}) copy-start(f32[1,64,768]{2,1,0:T(8,128)} %copy-done.41) | copy-start | bytes 589828
  578.6 24.5 %copy-start.172 = (f32[768]{0:T(1024)S(1)}, f32[768]{0:T(1024)}, u32[]{:S(2)}) copy-start(f32[768]{0:T(1024)} %get-tuple-element.33) | copy-start | bytes 9220
  578.6 24.5 %copy-start.210 = (f32[64]{0:T(128)S(1)}, f32[64]{0:T(128)}, u32[]{:S(2)}) copy-start(f32[64]{0:T(128)} %copy-done.209) | copy-start | bytes 772
  578.6 24.5 %copy-start.236 = (f32[64]{0:T(128)S(1)}, f32[64]{0:T(128)}, u32[]{:S(2)}) copy-start(f32[64]{0:T(128)} %copy-done.235) | copy-start | bytes 772
  578.6 34.3 %slice-start.12 = ((s8[4718592]{0:T(1024)(128)(4,1)}), s8[524288]{0:T(1024)(128)(4,1)S(1)}, s32[]{:S(2)}) async-start(s8[4718592]{0:T(1024)(128)(4,1)} %bitcast.654), calls=%async_computation.34 | async-start | bytes 1048576
  578.7 75.5 %reduce-scatter.35.cloned.1.call-start = ((), (), s32[]{:S(2)}) async-start(), calls=%async_computation.20 | async-start | bytes 983040
  580.7 26.5 %copy-start.112 = (bf16[12,64,64]{2,1,0:T(8,128)(2,1)}, bf16[12,64,64]{2,1,0:T(8,128)(2,1)S(1)}, u32[]{:S(2)}) copy-start(bf16[12,64,64]{2,1,0:T(8,128)(2,1)S(1)} %fusion.64) | copy-start | bytes 294916
  628.9 37.5 %slice-start.14 = ((s8[4718592]{0:T(1024)(128)(4,1)}), s8[524288]{0:T(1024)(128)(4,1)S(1)}, s32[]{:S(2)}) async-start(s8[4718592]{0:T(1024)(128)(4,1)} %bitcast.656), calls=%async_computation.36 | async-start | bytes 1048576
  631.3 24.5 %copy-start.40 = (f32[1,64,768]{2,1,0:T(8,128)S(1)}, f32[1,64,768]{2,1,0:T(8,128)}, u32[]{:S(2)}) copy-start(f32[1,64,768]{2,1,0:T(8,128)} %copy-done.38) | copy-start | bytes 589828
  631.3 24.5 %copy-start.175 = (f32[768]{0:T(1024)S(1)}, f32[768]{0:T(1024)}, u32[]{:S(2)}) copy-start(f32[768]{0:T(1024)} %get-tuple-element.34) | copy-start | bytes 9220
  631.3 24.5 %copy-start.208 = (f32[64]{0:T(128)S(1)}, f32[64]{0:T(128)}, u32[]{:S(2)}) copy-start(f32[64]{0:T(128)} %copy-done.207) | copy-start | bytes 772
  631.3 24.5 %copy-start.233 = (f32[64]{0:T(128)S(1)}, f32[64]{0:T(128)}, u32[]{:S(2)}) copy-start(f32[64]{0:T(128)} %copy-done.232) | copy-start | bytes 772
  631.4 71.7 %reduce-scatter.37.cloned.1.call-start = ((), (), s32[]{:S(2)}) async-start(), calls=%async_computation.21 | async-start | bytes 983040
  680.3 132.7 %reduce-scatter.23.cloned.1.call-start = ((), (), s32[]{:S(2)}) async-start(), calls=%async_computation.14 | async-start | bytes 2433024 | tf_op jit(solution)/shard_map/reduce_scatter | solution.py:257
  684.4 248.5 %reduce-scatter.21.cloned.1.call-start = ((), (), s32[]{:S(2)}) async-start(), calls=%async_computation.13 | async-start | bytes 7299072 | tf_op jit(solution)/shard_map/reduce_scatter | solution.py:256
  687.3 17.4 %copy-start.80 = (bf16[1,64,1536]{1,2,0:T(8,128)(2,1)S(1)}, bf16[1,64,1536]{1,2,0:T(8,128)(2,1)}, u32[]{:S(2)}) copy-start(bf16[1,64,1536]{1,2,0:T(8,128)(2,1)} %copy-done.79) | copy-start | bytes 589828
  690.0 20.6 %copy-start.124 = (bf16[12,64,64]{2,1,0:T(8,128)(2,1)}, bf16[12,64,64]{2,1,0:T(8,128)(2,1)S(1)}, u32[]{:S(2)}) copy-start(bf16[12,64,64]{2,1,0:T(8,128)(2,1)S(1)} %fusion.62) | copy-start | bytes 294916
  716.6 357.8 %reduce-scatter.25.cloned.1.call-start = ((), (), s32[]{:S(2)}) async-start(), calls=%async_computation.15 | async-start | bytes 9732096 | tf_op jit(solution)/shard_map/reduce_scatter | solution.py:258
  725.0 491.1 %reduce-scatter.27.cloned.1.call-start = ((), (), s32[]{:S(2)}) async-start(), calls=%async_computation.16 | async-start | bytes 9732096 | tf_op jit(solution)/shard_map/reduce_scatter | solution.py:259
  737.4 21.8 %copy-start.195 = (f32[768]{0:T(1024)S(1)}, f32[768]{0:T(1024)}, u32[]{:S(2)}) copy-start(f32[768]{0:T(1024)} %get-tuple-element.21) | copy-start | bytes 9220
  737.4 23.1 %copy-start.1 = (bf16[768,2304]{1,0:T(8,128)(2,1)S(1)}, bf16[768,2304]{1,0:T(8,128)(2,1)}, u32[]{:S(2)}) copy-start(bf16[768,2304]{1,0:T(8,128)(2,1)} %all-gather.6.cloned.1.call-done) | copy-start | bytes 10616836
  737.4 23.1 %copy-start.163 = (f32[768]{0:T(1024)S(1)}, f32[768]{0:T(1024)}, u32[]{:S(2)}) copy-start(f32[768]{0:T(1024)} %copy-done.161) | copy-start | bytes 9220
  737.4 23.1 %copy-start.194 = (f32[64]{0:T(128)S(1)}, f32[64]{0:T(128)}, u32[]{:S(2)}) copy-start(f32[64]{0:T(128)} %copy-done.192) | copy-start | bytes 772
  (250 other events, 798.0 us)
Sparse Core Ops, SparseCore 0:
  10.8 62.7 all-gather.5
  76.3 52.7 all-gather.7
  132.0 64.1 all-gather.9
  198.8 61.8 all-gather.11
  465.8 22.5 reduce-scatter.28
  522.3 22.6 reduce-scatter.30
  578.8 22.6 reduce-scatter.32
  631.5 22.6 reduce-scatter.34
  680.4 22.6 reduce-scatter.36
  708.8 99.1 reduce-scatter.22
  814.3 118.5 reduce-scatter.20
  939.2 135.2 reduce-scatter.24
  1080.9 135.1 reduce-scatter.26
where the time goes:
time: 1230 us; the launch traced here: 1220 us
  waiting for transfers between devices  588 us (48%)
  blocking collectives  257 us (21%)
  local copies, waits for them, and re-layouts  165 us (13%)
  matrix products  143 us (12%)
  other arithmetic  49.7 us (4%)
  between operations  18.7 us (2%)
    reduce_scatter x1, waiting for transfers between devices, on_device(): lax.psum_scatter(down_total, ('dp', 'ctx'), scatter_dimension=0, tiled=True)  142 us
    reduce_scatter x1, waiting for transfers between devices, on_device(): lax.psum_scatter(up_total, ('dp', 'ctx'), scatter_dimension=0, tiled=True)  142 us
    reduce_scatter x1, waiting for transfers between devices, on_device(): lax.psum_scatter(qkv_total, ('dp', 'ctx'), scatter_dimension=0, tiled=True)  120 us
    all_gather x5, blocking collectives, on_device(): kv_store.append(lax.all_gather(local_kv, 'ctx', axis=1, tiled=True))  102 us
    unnamed x621, local copies, waits for them, and re-layouts  98.2 us
    unnamed x18, waiting for transfers between devices  96 us
    unnamed x3, blocking collectives  90 us
    all_gather x1, blocking collectives, on_device(): lax.all_gather(pass_embed, ('dp', 'ctx'), axis=1, tiled=True)  64.6 us
  transfers between devices with their start and end apart: 13, of which 10 were waited for; matrix products, arithmetic and copies ran while one was open for 9% of the time, Pallas kernels for 0%

commit v1 on v0

--- a/solution.py
+++ b/solution.py
@@ -1,9 +1,266 @@
 import jax
 import jax.numpy as jnp
 from jax import lax
+from jax.experimental import pallas as pl
+from jax.experimental.pallas import tpu as pltpu
 from jax.sharding import PartitionSpec as P
 
 H = 12
+MESH = pl.DeviceIdType.MESH
+F32 = jnp.float32
+BF16 = jnp.bfloat16
+VMEM_LIMIT = 62 * 2**20
+
+
+def places():
+    dp = lax.axis_index("dp")
+    z = lax.axis_index("ctx")
+    partner = dp + 1 - 2 * lax.rem(dp, 2)
+    xdp = dp + 2 - 4 * lax.rem(dp // 2, 2)
+    ydp = dp + 4 - 8 * (dp // 4)
+    ddp = xdp + ydp - dp
+    return dp, z, partner, xdp, ydp, ddp
+
+
+def greet(dp, z, partner, xdp, ydp):
+    bar = pltpu.get_barrier_semaphore()
+    peers = [(partner, z), (xdp, z), (ydp, z)]
+    peers += [(dp, lax.rem(z + step, 4)) for step in (1, 2, 3)]
+    for peer in peers:
+        pl.semaphore_signal(bar, inc=1, device_id=peer, device_id_type=MESH)
+    pl.semaphore_wait(bar, len(peers))
+
+
+def halves(width):
+    first = (width // 256) * 128
+    return pl.ds(0, first), pl.ds(first, width - first)
+
+
+def gather_kernel(a_ref, b_ref, ao_ref, bo_ref, ssem, rsem, lsem):
+    dp, z, partner, xdp, ydp, ddp = places()
+    greet(dp, z, partner, xdp, ydp)
+    pend = []
+    pairs = ((a_ref, ao_ref), (b_ref, bo_ref))
+
+    def view(ref, block, half):
+        if half is None:
+            return ref.at[block]
+        return ref.at[block, :, halves(ref.shape[2])[half]]
+
+    def send(block, to, slot, own=False, half=None):
+        for t, (src, dst) in enumerate(pairs):
+            target = view(dst, block, half)
+            copy = pltpu.make_async_remote_copy(
+                src_ref=src if own else target,
+                dst_ref=target,
+                send_sem=ssem.at[t, len(pend) // 2],
+                recv_sem=rsem.at[t, slot],
+                device_id=to,
+                device_id_type=MESH,
+            )
+            copy.start()
+            pend.append(copy)
+
+    def wait(block, slot, half=None):
+        for t, (_, dst) in enumerate(pairs):
+            target = view(dst, block, half)
+            pltpu.make_async_remote_copy(
+                src_ref=target,
+                dst_ref=target,
+                send_sem=ssem.at[t, 0],
+                recv_sem=rsem.at[t, slot],
+                device_id=(partner, z),
+                device_id_type=MESH,
+            ).wait_recv()
+
+    zs = [lax.rem(z + 4 - step, 4) for step in range(4)]
+    me = dp * 4 + z
+    send(me, (xdp, z), 3, own=True)
+    send(me, (ydp, z), 7, own=True)
+    for step in (1, 2, 3):
+        send(me, (dp, lax.rem(z + step, 4)), step - 1, own=True)
+    send(me, (partner, z), 19, own=True)
+    local = [pltpu.make_async_copy(src, dst.at[me], lsem.at[t]) for t, (src, dst) in enumerate(pairs)]
+    for copy in local:
+        copy.start()
+
+    def relay(j):
+        bx, by = xdp * 4 + zs[j], ydp * 4 + zs[j]
+        wait(bx, 3 + j)
+        send(bx, (ydp, z), 11 + j, half=0)
+        send(bx, (partner, z), 23 + j)
+        wait(by, 7 + j)
+        send(by, (xdp, z), 15 + j, half=1)
+        send(by, (partner, z), 27 + j)
+
+    for j in range(1, 4):
+        block = dp * 4 + zs[j]
+        wait(block, j - 1)
+        send(block, (xdp, z), 3 + j)
+        send(block, (ydp, z), 7 + j)
+        send(block, (partner, z), 19 + j)
+        relay(j - 1)
+    relay(3)
+    for j in range(4):
+        block = ddp * 4 + zs[j]
+        wait(block, 11 + j, 0)
+        wait(block, 15 + j, 1)
+        send(block, (partner, z), 31 + j)
+    away = partner - dp
+    for first, column in ((19, dp), (23, xdp), (27, ydp), (31, ddp)):
+        for j in range(4):
+            wait((column + away) * 4 + zs[j], first + j)
+    for copy in local:
+        copy.wait()
+    for copy in pend:
+        copy.wait_send()
+
+
+def gather_blocks(a, b):
+    count = lax.axis_size("dp") * lax.axis_size("ctx")
+    return pl.pallas_call(
+        gather_kernel,
+        out_shape=(
+            jax.ShapeDtypeStruct((count,) + a.shape, a.dtype),
+            jax.ShapeDtypeStruct((count,) + b.shape, b.dtype),
+        ),
+        in_specs=[pl.BlockSpec(memory_space=pltpu.VMEM)] * 2,
+        out_specs=[pl.BlockSpec(memory_space=pl.ANY)] * 2,
+        scratch_shapes=[
+            pltpu.SemaphoreType.DMA((2, 35)),
+            pltpu.SemaphoreType.DMA((2, 35)),
+            pltpu.SemaphoreType.DMA((2,)),
+        ],
+        compiler_params=pltpu.CompilerParams(collective_id=0, has_side_effects=True),
+    )(a, b)
+
+
+def reduce_kernel(
+    a_hbm, b_hbm, ao_ref, bo_ref,
+    la, lb, pa, pb, fxa, fxb, fya, fyb, hxa, hxb, hya, hyb, za, zb,
+    lsem, ssem, rsem,
+):
+    dp, z, partner, xdp, ydp, ddp = places()
+    greet(dp, z, partner, xdp, ydp)
+    pend = []
+
+    def send(sources, targets, to, slot):
+        for t in (0, 1):
+            copy = pltpu.make_async_remote_copy(
+                src_ref=sources[t],
+                dst_ref=targets[t],
+                send_sem=ssem.at[t, len(pend) // 2],
+                recv_sem=rsem.at[t, slot],
+                device_id=to,
+                device_id_type=MESH,
+            )
+            copy.start()
+            pend.append(copy)
+
+    def wait(targets, slot):
+        for t in (0, 1):
+            pltpu.make_async_remote_copy(
+                src_ref=targets[t],
+                dst_ref=targets[t],
+                send_sem=ssem.at[t, 0],
+                recv_sem=rsem.at[t, slot],
+                device_id=(partner, z),
+                device_id_type=MESH,
+            ).wait_recv()
+
+    zs = [lax.rem(z + 1 + j, 4) for j in range(4)]
+    columns = (ddp, xdp, ydp, dp)
+    order = [(0, 0), (0, 1), (1, 0), (2, 0), (0, 2), (1, 1), (2, 1), (3, 0)]
+    order += [(0, 3), (1, 2), (2, 2), (3, 1), (1, 3), (2, 3), (3, 2), (3, 3)]
+    loads = {}
+    for c, j in order:
+        s = c * 4 + j
+        block = columns[c] * 4 + zs[j]
+        other = block + (partner - dp) * 4
+        send((a_hbm.at[other], b_hbm.at[other]), (pa.at[s], pb.at[s]), (partner, z), s)
+        loads[s] = [
+            pltpu.make_async_copy(src.at[block], dst.at[s], lsem.at[t, s])
+            for t, (src, dst) in enumerate(((a_hbm, la), (b_hbm, lb)))
+        ]
+        for copy in loads[s]:
+            copy.start()
+    a_half = halves(a_hbm.shape[2])
+    b_half = halves(b_hbm.shape[2])
+    for c, j in order:
+        s = c * 4 + j
+        for copy in loads[s]:
+            copy.wait()
+        wait((pa.at[s], pb.at[s]), s)
+        if c == 0:
+            for mine, other in ((la, pa), (lb, pb)):
+                mine[s] = (mine[s].astype(F32) + other[s].astype(F32)).astype(mine.dtype)
+            send((la.at[s, :, a_half[0]], lb.at[s, :, b_half[0]]), (hxa.at[j], hxb.at[j]), (xdp, z), 16 + j)
+            send((la.at[s, :, a_half[1]], lb.at[s, :, b_half[1]]), (hya.at[j], hyb.at[j]), (ydp, z), 20 + j)
+        elif c < 3:
+            got, slot, part = ((hya, hyb), 20, 1) if c == 1 else ((hxa, hxb), 16, 0)
+            wait((got[0].at[j], got[1].at[j]), slot + j)
+            for mine, other, extra, half in ((la, pa, got[0], a_half), (lb, pb, got[1], b_half)):
+                plain, joined = half[1 - part], half[part]
+                mine[s, :, plain] = (mine[s, :, plain].astype(F32) + other[s, :, plain].astype(F32)).astype(mine.dtype)
+                mine[s, :, joined] = (
+                    mine[s, :, joined].astype(F32) + other[s, :, joined].astype(F32) + extra[j].astype(F32)
+                ).astype(mine.dtype)
+            into, to, slot = ((fxa, fxb), xdp, 24) if c == 1 else ((fya, fyb), ydp, 28)
+            send((la.at[s], lb.at[s]), (into[0].at[j], into[1].at[j]), (to, z), slot + j)
+        else:
+            wait((fxa.at[j], fxb.at[j]), 24 + j)
+            wait((fya.at[j], fyb.at[j]), 28 + j)
+            totals = [
+                mine[s].astype(F32) + other[s].astype(F32) + first[j].astype(F32) + second[j].astype(F32)
+                for mine, other, first, second in ((la, pa, fxa, fya), (lb, pb, fxb, fyb))
+            ]
+            if j < 3:
+                la[s] = totals[0].astype(la.dtype)
+                lb[s] = totals[1].astype(lb.dtype)
+                send((la.at[s], lb.at[s]), (za.at[j], zb.at[j]), (dp, zs[j]), 32 + j)
+            else:
+                ao_ref[...] = totals[0]
+                bo_ref[...] = totals[1]
+    for j in range(3):
+        wait((za.at[j], zb.at[j]), 32 + j)
+        ao_ref[...] += za[j].astype(F32)
+        bo_ref[...] += zb[j].astype(F32)
+    for copy in pend:
+        copy.wait_send()
+
+
+def reduce_blocks(a, b):
+    _, ra, ca = a.shape
+    _, rb, cb = b.shape
+    ha, hb = (ca // 256) * 128, (cb // 256) * 128
+
+    def buffers(count, first, second):
+        return [
+            pltpu.VMEM((count, ra, ca if first is None else first), a.dtype),
+            pltpu.VMEM((count, rb, cb if second is None else second), b.dtype),
+        ]
+
+    return pl.pallas_call(
+        reduce_kernel,
+        out_shape=(jax.ShapeDtypeStruct((ra, ca), F32), jax.ShapeDtypeStruct((rb, cb), F32)),
+        in_specs=[pl.BlockSpec(memory_space=pl.ANY)] * 2,
+        out_specs=[pl.BlockSpec(memory_space=pltpu.VMEM)] * 2,
+        scratch_shapes=buffers(16, None, None)
+        + buffers(16, None, None)
+        + buffers(4, None, None)
+        + buffers(4, None, None)
+        + buffers(4, ha, hb)
+        + buffers(4, ca - ha, cb - hb)
+        + buffers(3, None, None)
+        + [
+            pltpu.SemaphoreType.DMA((2, 16)),
+            pltpu.SemaphoreType.DMA((2, 35)),
+            pltpu.SemaphoreType.DMA((2, 35)),
+        ],
+        compiler_params=pltpu.CompilerParams(
+            collective_id=1, has_side_effects=True, vmem_limit_bytes=VMEM_LIMIT
+        ),
+    )(a, b)
 
 
 def layer_norm(entry, gain_row, shift_row):
@@ -93,29 +350,25 @@
     first_backs = []
     second_backs = []
     gelu_backs = []
+    small_in = jnp.stack([attn_gain, attn_shift, ffn_gain, ffn_shift], axis=1)
+    small_in = jnp.concatenate([small_in, pass_embed.T], axis=1)
+    small_in = jnp.pad(small_in, ((0, 0), (0, 128 - small_in.shape[1])))
+    rows_a = jnp.concatenate([qkv_weight, out_weight, up_weight, small_in], axis=1)
+    if (lax.axis_size("dp"), lax.axis_size("ctx")) == (8, 4):
+        all_a, all_b = gather_blocks(rows_a, down_weight)
+    else:
+        all_a = lax.all_gather(rows_a, ("dp", "ctx"), axis=0)
+        all_b = lax.all_gather(down_weight, ("dp", "ctx"), axis=0)
+    all_a = all_a.reshape(model_width, -1)
+    down_full = all_b.reshape(-1, model_width)
+    qkv_cols, ff_width = qkv_weight.shape[1], up_weight.shape[1]
+    qkv_full = all_a[:, :qkv_cols]
+    out_full = all_a[:, qkv_cols : qkv_cols + model_width]
+    up_full = all_a[:, qkv_cols + model_width : qkv_cols + model_width + ff_width]
+    small_rows = all_a[:, qkv_cols + model_width + ff_width :].T
+    gain_first, shift_first, gain_second, shift_second = (small_rows[row] for row in range(4))
+    embed_full = small_rows[4 : 4 + repeats]
     for repeat in range(repeats):
-        params = (
-            lax.all_gather(qkv_weight, ("dp", "ctx"), axis=0, tiled=True),
-            lax.all_gather(out_weight, ("dp", "ctx"), axis=0, tiled=True),
-            lax.all_gather(up_weight, ("dp", "ctx"), axis=0, tiled=True),
-            lax.all_gather(down_weight, ("dp", "ctx"), axis=0, tiled=True),
-            lax.all_gather(attn_gain, ("dp", "ctx"), axis=0, tiled=True),
-            lax.all_gather(attn_shift, ("dp", "ctx"), axis=0, tiled=True),
-            lax.all_gather(ffn_gain, ("dp", "ctx"), axis=0, tiled=True),
-            lax.all_gather(ffn_shift, ("dp", "ctx"), axis=0, tiled=True),
-            lax.all_gather(pass_embed, ("dp", "ctx"), axis=1, tiled=True),
-        )
-        (
-            qkv_full,
-            out_full,
-            up_full,
-            down_full,
-            gain_first,
-            shift_first,
-            gain_second,
-            shift_second,
-            embed_full,
-        ) = params
         entry = current + embed_full[repeat].astype(jnp.float32)
         normed, norm_first_back = jax.vjp(
             layer_norm, entry, gain_first.astype(jnp.float32), shift_first.astype(jnp.float32)
@@ -165,28 +418,6 @@
     carry = jnp.zeros((seq_count, local_tok, model_width), jnp.float32)
     cot_split = cotangent.reshape(seq_count, local_tok, repeats, model_width)
     for repeat in reversed(range(repeats)):
-        params = (
-            lax.all_gather(qkv_weight, ("dp", "ctx"), axis=0, tiled=True),
-            lax.all_gather(out_weight, ("dp", "ctx"), axis=0, tiled=True),
-            lax.all_gather(up_weight, ("dp", "ctx"), axis=0, tiled=True),
-            lax.all_gather(down_weight, ("dp", "ctx"), axis=0, tiled=True),
-            lax.all_gather(attn_gain, ("dp", "ctx"), axis=0, tiled=True),
-            lax.all_gather(attn_shift, ("dp", "ctx"), axis=0, tiled=True),
-            lax.all_gather(ffn_gain, ("dp", "ctx"), axis=0, tiled=True),
-            lax.all_gather(ffn_shift, ("dp", "ctx"), axis=0, tiled=True),
-            lax.all_gather(pass_embed, ("dp", "ctx"), axis=1, tiled=True),
-        )
-        (
-            qkv_full,
-            out_full,
-            up_full,
-            down_full,
-            gain_first,
-            shift_first,
-            gain_second,
-            shift_second,
-            embed_full,
-        ) = params
         grad_out = cot_split[:, :, repeat].astype(jnp.float32) + carry
         queries = query_keep[repeat]
         key_heads, value_heads = stored_keys(kv_store, repeat + 1, model_width, head_count)
@@ -252,16 +483,28 @@
     up_total = outer_sum(normed_mid_keep, hidden_keep)
     down_total = outer_sum(activated_keep, branch_keep)
     embed_grad = jnp.stack(embed_rows, axis=0)
+    small_total = jnp.concatenate([jnp.stack(small_totals, axis=0), embed_grad], axis=0).T
+    small_total = jnp.pad(small_total, ((0, 0), (0, 128 - small_total.shape[1])))
+    grad_a = jnp.concatenate(
+        [qkv_total.astype(jnp.bfloat16), out_total.astype(jnp.bfloat16), up_total.astype(jnp.bfloat16), small_total.astype(jnp.bfloat16)], axis=1
+    ).reshape(-1, *rows_a.shape)
+    grad_b = down_total.astype(jnp.bfloat16).reshape(-1, *down_weight.shape)
+    if (lax.axis_size("dp"), lax.axis_size("ctx")) == (8, 4):
+        own_a, own_b = reduce_blocks(grad_a, grad_b)
+    else:
+        own_a = lax.psum_scatter(grad_a.astype(jnp.float32), ("dp", "ctx"), scatter_dimension=0)
+        own_b = lax.psum_scatter(grad_b.astype(jnp.float32), ("dp", "ctx"), scatter_dimension=0)
+    own_small = own_a[:, qkv_cols + model_width + ff_width :].T
     reduced = (
-        lax.psum_scatter(qkv_total, ("dp", "ctx"), scatter_dimension=0, tiled=True),
-        lax.psum_scatter(out_total, ("dp", "ctx"), scatter_dimension=0, tiled=True),
-        lax.psum_scatter(up_total, ("dp", "ctx"), scatter_dimension=0, tiled=True),
-        lax.psum_scatter(down_total, ("dp", "ctx"), scatter_dimension=0, tiled=True),
-        lax.psum_scatter(small_totals[0], ("dp", "ctx"), scatter_dimension=0, tiled=True),
-        lax.psum_scatter(small_totals[1], ("dp", "ctx"), scatter_dimension=0, tiled=True),
-        lax.psum_scatter(small_totals[2], ("dp", "ctx"), scatter_dimension=0, tiled=True),
-        lax.psum_scatter(small_totals[3], ("dp", "ctx"), scatter_dimension=0, tiled=True),
-        lax.psum_scatter(embed_grad, ("dp", "ctx"), scatter_dimension=1, tiled=True),
+        own_a[:, :qkv_cols],
+        own_a[:, qkv_cols : qkv_cols + model_width],
+        own_a[:, qkv_cols + model_width : qkv_cols + model_width + ff_width],
+        own_b,
+        own_small[0],
+        own_small[1],
+        own_small[2],
+        own_small[3],
+        own_small[4 : 4 + repeats],
     )
     activations = jnp.stack(pass_outputs, axis=2).reshape(
         seq_count, local_tok * repeats, model_width

time: 1230 us -> 763 us (0.62)
  waiting for transfers between devices: 588 us -> 36.9 us
  blocking collectives: 257 us -> 101 us
  Pallas kernels: 0 us -> 148 us
  other arithmetic: 49.7 us -> 82.3 us
  matrix products: 143 us -> 173 us
  local copies, waits for them, and re-layouts: 165 us -> 192 us
    reduce_scatter x4 -> x0, waiting for transfers between devices: 403 us -> none  [the longest x1 142 us: on_device(): lax.psum_scatter(down_total, ('dp', 'ctx'), scatter_dimension=0, tiled=True)]
    pallas_call x0 -> x2, Pallas kernels: none -> 148 us  [the longest x1 74.6 us: gather_blocks(): pl.pallas_call(gather_kernel, out_shape=(jax.ShapeDtypeStruct((count,) +...]
    all_gather x4 -> x0, waiting for transfers between devices: 88.9 us -> none  [the longest x1 60.1 us: on_device(): lax.all_gather(down_weight, ('dp', 'ctx'), axis=0, tiled=True)]
    unnamed x3 -> x1, blocking collectives: 90 us -> 16.3 us
    all_gather x1 -> x0, blocking collectives: 64.6 us -> none  [on_device(): lax.all_gather(pass_embed, ('dp', 'ctx'), axis=1, tiled=True)]
    unnamed x18 -> x10, waiting for transfers between devices: 96 us -> 36.9 us
    dot_general x20, matrix products: 51.3 us -> 70.6 us  [project_back(): jnp.einsum('ste,de->std', features, matrix, preferred_element_type=jnp.fl...]
    all_gather x5, blocking collectives: 102 us -> 84.5 us  [on_device(): kv_store.append(lax.all_gather(local_kv, 'ctx', axis=1, tiled=True))]
  transfers between devices with their start and end apart: 13 -> 5, of which waited for: 10 -> 4; matrix products, arithmetic and copies ran while one was open for 9% -> 10% of each run, Pallas kernels for 0% -> 0%
where the time goes in v1:
time: 763 us; the launch traced here: 753 us
  local copies, waits for them, and re-layouts  192 us (25%)
  matrix products  173 us (23%)
  Pallas kernels  148 us (19%)
  blocking collectives  101 us (13%)
  other arithmetic  82.3 us (11%)
  waiting for transfers between devices  36.9 us (5%)
  between operations  18 us (2%)
    unnamed x544, local copies, waits for them, and re-layouts  106 us
    all_gather x5, blocking collectives, on_device(): kv_store.append(lax.all_gather(local_kv, 'ctx', axis=1, tiled=True))  84.5 us
    pallas_call x1, Pallas kernels, gather_blocks(): pl.pallas_call(gather_kernel, out_shape=(jax.ShapeDtypeStruct((count,) +...  74.6 us
    pallas_call x1, Pallas kernels, reduce_blocks(): pl.pallas_call(reduce_kernel, out_shape=(jax.ShapeDtypeStruct((ra, ca), F...  73.8 us
    dot_general x20, matrix products, project_back(): jnp.einsum('ste,de->std', features, matrix, preferred_element_type=jnp.fl...  70.6 us
    dot_general x20, matrix products, project(): jnp.einsum('std,de->ste', features, matrix, preferred_element_type=jnp.fl...  40 us
    unnamed x10, waiting for transfers between devices  36.9 us
    slice x10, local copies, waits for them, and re-layouts, stored_keys(): joined[:, :, :model_width]  20.4 us
  transfers between devices with their start and end apart: 5, of which 4 were waited for; matrix products, arithmetic and copies ran while one was open for 10% of the time, Pallas kernels for 0%

profile of v1, /device:TPU:0, one launch (start us, length us, event | category | flops | bytes accessed | tf_op | source)
XLA Modules:
  0.0 753.2 jit_solution(11028474947221905569)
XLA Ops:
  12.8 74.6 %shard_map.203 = (bf16[32,24,6272]{2,1,0:T(8,128)(2,1)}, bf16[32,96,768]{2,1,0:T(8,128)(2,1)}) custom-call(bf16[24,6272]{1,0:T(8,128)(2,1)} %fusion.147.a_ref, bf16[96,768]{1,0:T(8,128)(2,1)} %b_ref.1), custom_call_target="tpu_custom_call" | custom-call | tf_op jit(solution)/shard_map/pallas_call | solution.py:121
  95.7 16.3 %all-reduce.2 = s32[256]{0:T(256)S(1)} all-reduce(s32[256]{0:T(256)S(1)} %bitcast_dynamic-update-slice_fusion.10), channel_id=1, replica_groups=mesh['dp'=8,'ctx'=4] {'ctx'}, use_global_device_ids=true, to_apply=%add.2 | all-reduce | flops 256 | bytes 2048
  112.1 17.7 %all_gather.20 = bf16[1,256,1536]{2,1,0:T(8,128)(2,1)S(1)} all-gather(bf16[1,64,1536]{2,1,0:T(8,128)(2,1)S(1)} %slice.266), channel_id=1, replica_groups=mesh['dp'=8,'ctx'=4] {'ctx'}, dimensions={1}, use_global_device_ids=true | all-gather | bytes 983040 | tf_op jit(solution)/shard_map/all_gather | solution.py:379
  133.9 4.3 bitcast_dynamic-update-slice_fusion.4
  148.1 17.8 %all_gather.23 = bf16[1,256,1536]{2,1,0:T(8,128)(2,1)S(1)} all-gather(bf16[1,64,1536]{2,1,0:T(8,128)(2,1)} %slice.275), channel_id=1, replica_groups=mesh['dp'=8,'ctx'=4] {'ctx'}, dimensions={1}, use_global_device_ids=true | all-gather | bytes 983040 | tf_op jit(solution)/shard_map/all_gather | solution.py:379
  167.7 3.5 fusion.295
  179.0 4.3 bitcast_dynamic-update-slice_fusion.3
  185.4 2.9 fusion.6
  188.7 16.6 %all_gather.24 = bf16[1,256,1536]{2,1,0:T(8,128)(2,1)S(1)} all-gather(bf16[1,64,1536]{2,1,0:T(8,128)(2,1)S(1)} %slice.280), channel_id=1, replica_groups=mesh['dp'=8,'ctx'=4] {'ctx'}, dimensions={1}, use_global_device_ids=true | all-gather | bytes 983040 | tf_op jit(solution)/shard_map/all_gather | solution.py:379
  225.1 16.1 %all_gather.25 = bf16[1,256,1536]{2,1,0:T(8,128)(2,1)S(1)} all-gather(bf16[1,64,1536]{2,1,0:T(8,128)(2,1)S(1)} %slice.285), channel_id=1, replica_groups=mesh['dp'=8,'ctx'=4] {'ctx'}, dimensions={1}, use_global_device_ids=true | all-gather | bytes 983040 | tf_op jit(solution)/shard_map/all_gather | solution.py:379
  265.2 4.5 fusion.296
  271.4 16.3 %all_gather.26 = bf16[1,256,1536]{2,1,0:T(8,128)(2,1)S(1)} all-gather(bf16[1,64,1536]{2,1,0:T(8,128)(2,1)} %slice.290), channel_id=1, replica_groups=mesh['dp'=8,'ctx'=4] {'ctx'}, dimensions={1}, use_global_device_ids=true | all-gather | bytes 983040 | tf_op jit(solution)/shard_map/all_gather | solution.py:379
  288.6 4.3 fusion.292
  293.0 4.0 copy.142
  297.0 4.0 copy.141
  321.5 4.0 multiply_reduce_fusion
  331.7 4.8 copy.168
  340.5 3.5 fusion.62
  344.0 18.1 %reduce-scatter.16.cloned.1.call-done = bf16[64,1536]{1,0:T(8,128)(2,1)} async-done(((bf16[256,1536]{1,0:T(8,128)(2,1)}), bf16[64,1536]{1,0:T(8,128)(2,1)}) %reduce-scatter.16.cloned.1.call-update) | async-done | bytes 196624
  366.0 4.3 fusion.157
  371.3 4.0 fusion.105
  375.4 4.6 fusion.151
  397.1 4.8 copy.170
  406.1 4.2 fusion.77
  419.6 3.1 fusion.60
  422.8 4.3 reduce-scatter.18.cloned.1.call-done
  430.9 4.1 fusion.156
  436.1 4.0 fusion.98
  440.2 4.6 fusion.150
  460.9 4.8 copy.172
  480.8 10.2 %reduce-scatter.20.cloned.1.call-done = bf16[64,1536]{1,0:T(8,128)(2,1)} async-done(((bf16[256,1536]{1,0:T(8,128)(2,1)}), bf16[64,1536]{1,0:T(8,128)(2,1)}) %reduce-scatter.20.cloned.1.call-update) | async-done | bytes 196624
  494.9 4.2 fusion.155
  500.2 4.0 fusion.91
  504.2 4.6 fusion.149
  524.4 4.8 copy.174
  559.1 4.1 fusion.154
  564.3 4.7 bitcast_dynamic-update-slice_fusion.9
  569.1 5.2 fusion.148
  602.9 3.3 fusion.45
  606.3 3.7 copy.176
  617.3 6.6 convolution_convert_fusion.1
  624.0 5.6 convolution_convert_fusion.2
  629.6 4.2 reduce-scatter.24.cloned.1.call-done
  636.4 3.4 fusion.158
  647.2 4.8 concatenate.215
  652.1 3.7 convolution_convert_fusion
  655.8 8.1 %fusion.1 = bf16[768,6272]{1,0:T(8,128)(2,1)} fusion(bf16[768,9]{1,0:T(8,128)(2,1)S(1)} %bitcast.763, bf16[768,3072]{1,0:T(8,128)(2,1)} %convolution_convert_fusion.2, bf16[768,768]{1,0:T(8,128)(2,1)S(1)} %copy.166, bf16[768,2304]{1,0:T(8,128)(2,1)S(1)} %convolution_convert_fusion), kind=kLoop, calls=%fused_computation.10 | loop fusion | flops 48168960 | bytes 19084800 | tf_op jit(solution)/shard_map/concatenate | solution.py:488
  663.9 73.8 %shard_map.204 = (f32[24,6272]{1,0:T(8,128)}, f32[96,768]{1,0:T(8,128)}) custom-call(bf16[32,24,6272]{2,1,0:T(8,128)(2,1)} %bitcast.657, bf16[32,96,768]{2,1,0:T(8,128)(2,1)} %bitcast.722), custom_call_target="tpu_custom_call" | custom-call | tf_op jit(solution)/shard_map/pallas_call | solution.py:243
  (807 shorter events, 291.5 us)
Async XLA Ops:
  7.2 354.9 %reduce-scatter.16.cloned.1.call-start = ((), (), s32[]{:S(2)}) async-start(), calls=%async_computation.5 | async-start | bytes 983040
  89.2 51.1 %copy-start.135 = (f32[768]{0:T(1024)}, f32[768]{0:T(1024)S(1)}, u32[]{:S(2)}) copy-start(f32[768]{0:T(1024)S(1)} %get-tuple-element.78) | copy-start | bytes 9220
  89.2 51.1 %copy-start.138 = (f32[768]{0:T(1024)}, f32[768]{0:T(1024)S(1)}, u32[]{:S(2)}) copy-start(f32[768]{0:T(1024)S(1)} %get-tuple-element.75) | copy-start | bytes 9220
  112.1 18.6 %copy-start.83 = (bf16[1,64,768]{1,2,0:T(8,128)(2,1)}, bf16[1,64,768]{1,2,0:T(8,128)(2,1)S(1)}, u32[]{:S(2)}) copy-start(bf16[1,64,768]{1,2,0:T(8,128)(2,1)S(1)} %copy.189) | copy-start | bytes 294916
  130.3 16.0 %copy-start.123 = (pred[64,256]{1,0:T(8,128)(4,1)}, pred[64,256]{1,0:T(8,128)(4,1)S(1)}, u32[]{:S(2)}) copy-start(pred[64,256]{1,0:T(8,128)(4,1)S(1)} %fusion.213) | copy-start | bytes 49156
  131.6 6.6 copy-start.96
  131.8 6.5 slice-start
  148.1 26.2 %copy-start.75 = (bf16[1,64,768]{1,2,0:T(8,128)(2,1)}, bf16[1,64,768]{1,2,0:T(8,128)(2,1)S(1)}, u32[]{:S(2)}) copy-start(bf16[1,64,768]{1,2,0:T(8,128)(2,1)S(1)} %copy.190) | copy-start | bytes 294916
  176.8 6.5 copy-start.108
  176.9 6.5 slice-start.2
  185.0 29.9 %copy-start.33 = (f32[1,64,768]{2,1,0:T(8,128)}, f32[1,64,768]{2,1,0:T(8,128)S(1)}, u32[]{:S(2)}) copy-start(f32[1,64,768]{2,1,0:T(8,128)S(1)} %get-tuple-element.155) | copy-start | bytes 589828
  185.4 19.9 %copy-start.52 = (bf16[1,768,1536]{2,1,0:T(8,128)(2,1)S(1)}, bf16[1,768,1536]{2,1,0:T(8,128)(2,1)}, u32[]{:S(2)}) copy-start(bf16[1,768,1536]{2,1,0:T(8,128)(2,1)} %copy-done.51) | copy-start | bytes 7077892
  188.7 24.0 %copy-start.77 = (bf16[1,64,768]{1,2,0:T(8,128)(2,1)}, bf16[1,64,768]{1,2,0:T(8,128)(2,1)S(1)}, u32[]{:S(2)}) copy-start(bf16[1,64,768]{1,2,0:T(8,128)(2,1)S(1)} %copy.191) | copy-start | bytes 294916
  208.2 6.8 slice-start.10
  247.8 6.5 slice-start.13
  250.2 135.3 %copy-start.16 = (f32[12,64,1024]{2,1,0:T(8,128)}, f32[12,64,1024]{2,1,0:T(8,128)S(1)}, u32[]{:S(2)}) copy-start(f32[12,64,1024]{2,1,0:T(8,128)S(1)} %get-tuple-element.163) | copy-start | bytes 9437188
  303.4 9.8 %slice-start.8 = ((s8[4718592]{0:T(1024)(128)(4,1)}), s8[4194304]{0:T(1024)(128)(4,1)S(1)}, s32[]{:S(2)}) async-start(s8[4718592]{0:T(1024)(128)(4,1)} %bitcast.646), calls=%async_computation.18 | async-start | bytes 8388608
  306.4 6.9 slice-start.9
  307.3 6.0 copy-start.112
  311.2 5.9 copy-start.47
  311.2 5.9 copy-start.187
  311.4 5.7 copy-start.209
  339.0 88.1 %reduce-scatter.18.cloned.1.call-start = ((), (), s32[]{:S(2)}) async-start(), calls=%async_computation.6 | async-start | bytes 983040
  365.9 5.3 copy-start.89
  366.0 5.3 copy-start.120
  404.3 86.7 %reduce-scatter.20.cloned.1.call-start = ((), (), s32[]{:S(2)}) async-start(), calls=%async_computation.7 | async-start | bytes 983040
  453.9 5.8 copy-start.7
  468.2 86.9 %reduce-scatter.22.cloned.1.call-start = ((), (), s32[]{:S(2)}) async-start(), calls=%async_computation.8 | async-start | bytes 983040
  494.8 5.2 copy-start.87
  494.8 5.3 copy-start.116
  514.3 6.3 copy-start.14
  531.6 102.2 %reduce-scatter.24.cloned.1.call-start = ((), (), s32[]{:S(2)}) async-start(), calls=%async_computation.9 | async-start | bytes 983040
  534.4 14.8 %copy-start.106 = (f32[64,768]{1,0:T(8,128)S(1)}, f32[64,768]{1,0:T(8,128)}, u32[]{:S(2)}) copy-start(f32[64,768]{1,0:T(8,128)} %copy-done.105) | copy-start | bytes 589828
  549.2 9.8 %copy-start.140 = (f32[768]{0:T(1024)S(1)}, f32[768]{0:T(1024)}, u32[]{:S(2)}) copy-start(f32[768]{0:T(1024)} %copy-done.138) | copy-start | bytes 9220
  559.1 5.2 copy-start.114
  569.1 5.2 copy-start.215
  579.4 16.0 %copy-start.62 = (f32[1,64,768]{2,1,0:T(8,128)S(1)}, f32[1,64,768]{2,1,0:T(8,128)}, u32[]{:S(2)}) copy-start(f32[1,64,768]{2,1,0:T(8,128)} %copy-done.60) | copy-start | bytes 589828
  583.6 19.3 %copy-start.15 = (f32[12,64,1024]{2,1,0:T(8,128)S(1)}, f32[12,64,1024]{2,1,0:T(8,128)}, u32[]{:S(2)}) copy-start(f32[12,64,1024]{2,1,0:T(8,128)} %copy-done.12) | copy-start | bytes 9437188
  586.9 16.0 %copy-start.9 = (f32[12,64,1280]{2,1,0:T(8,128)S(1)}, f32[12,64,1280]{2,1,0:T(8,128)}, u32[]{:S(2)}) copy-start(f32[12,64,1280]{2,1,0:T(8,128)} %copy-done.5) | copy-start | bytes 11796484
  588.1 8.0 %copy-start.59 = (f32[1,64,768]{2,1,0:T(8,128)S(1)}, f32[1,64,768]{2,1,0:T(8,128)}, u32[]{:S(2)}) copy-start(f32[1,64,768]{2,1,0:T(8,128)} %copy-done.57) | copy-start | bytes 589828
  589.3 13.6 %copy-start.4 = (f32[12,64,1280]{2,1,0:T(8,128)S(1)}, f32[12,64,1280]{2,1,0:T(8,128)}, u32[]{:S(2)}) copy-start(f32[12,64,1280]{2,1,0:T(8,128)} %copy-done) | copy-start | bytes 11796484
  617.3 6.7 copy-start.127
  617.3 6.7 copy-start.231
  624.0 12.4 %copy-start.54 = (bf16[1,64,768]{2,1,0:T(8,128)(2,1)S(1)}, bf16[1,64,768]{2,1,0:T(8,128)(2,1)}, u32[]{:S(2)}) copy-start(bf16[1,64,768]{2,1,0:T(8,128)(2,1)} %param.12) | copy-start | bytes 294916
  624.0 12.4 %copy-start.111 = (bf16[12,64,64]{2,1,0:T(8,128)(2,1)S(1)}, bf16[12,64,64]{2,1,0:T(8,128)(2,1)}, u32[]{:S(2)}) copy-start(bf16[12,64,64]{2,1,0:T(8,128)(2,1)} %fusion.61) | copy-start | bytes 294916
  624.0 12.4 %copy-start.169 = (f32[64]{0:T(128)S(1)}, f32[64]{0:T(128)}, u32[]{:S(2)}) copy-start(f32[64]{0:T(128)} %copy-done.168) | copy-start | bytes 772
  639.8 7.4 copy-start.68
  639.8 7.4 copy-start.69
  (209 other events, 612.3 us)
Sparse Core Ops, SparseCore 0:
  339.1 22.9 reduce-scatter.15
  404.4 22.6 reduce-scatter.17
  468.3 22.6 reduce-scatter.19
  531.7 22.6 reduce-scatter.21
  611.1 22.6 reduce-scatter.23

commit v2 on v1

--- a/solution.py
+++ b/solution.py
@@ -263,55 +263,378 @@
     )(a, b)
 
 
-def layer_norm(entry, gain_row, shift_row):
-    row_mean = jnp.mean(entry, axis=-1, keepdims=True)
-    centered = entry - row_mean
-    variance = jnp.mean(centered * centered, axis=-1, keepdims=True)
-    return centered * lax.rsqrt(variance + 1e-05) * gain_row + shift_row
-
-
-def gelu_tanh(values):
-    return jax.nn.gelu(values, approximate=True)
-
-
-def project(features, matrix):
-    return jnp.einsum("std,de->ste", features, matrix, preferred_element_type=jnp.float32)
-
-
-def project_back(features, matrix):
-    return jnp.einsum("ste,de->std", features, matrix, preferred_element_type=jnp.float32)
-
-
-def outer_sum(feature_list, grad_list):
-    features = jnp.concatenate(feature_list, axis=1)
-    grads_in = jnp.concatenate(grad_list, axis=1)
-    return jnp.einsum("std,ste->de", features, grads_in, preferred_element_type=jnp.float32)
-
-
-def split_heads(tensor, head_count):
-    return tensor.reshape(
-        tensor.shape[0], tensor.shape[1], head_count, tensor.shape[2] // head_count
+def ring():
+    dp = lax.axis_index("dp")
+    z = lax.axis_index("ctx")
+    size = lax.axis_size("ctx")
+    return z, (dp, lax.rem(z + 1, size)), (dp, lax.rem(z + size - 1, size))
+
+
+def mm(x, w):
+    return jnp.dot(x, w, preferred_element_type=F32)
+
+
+def mm_nt(x, w):
+    return lax.dot_general(x, w, (((1,), (1,)), ((), ())), preferred_element_type=F32)
+
+
+def mm_tn(x, w):
+    return lax.dot_general(x, w, (((0,), (0,)), ((), ())), preferred_element_type=F32)
+
+
+def row_mean(values):
+    return jnp.mean(values, axis=-1, keepdims=True)
+
+
+def norm_forward(entry):
+    centered = entry - row_mean(entry)
+    scale = lax.rsqrt(row_mean(centered * centered) + 1e-05)
+    return centered * scale, scale
+
+
+def norm_backward(grad, gain, unit, scale):
+    e = grad * gain
+    return (e - row_mean(e) - unit * row_mean(e * unit)) * scale
+
+
+def split_pair(pair):
+    lane = lax.broadcasted_iota(jnp.int32, pair.shape, 1)
+    zero = jnp.zeros_like(pair)
+    return jnp.concatenate([jnp.where(lane < 64, pair, zero), jnp.where(lane < 64, zero, pair)], axis=0)
+
+
+def join_pair(both):
+    half = both.shape[0] // 2
+    lane = lax.broadcasted_iota(jnp.int32, (half, 128), 1)
+    return jnp.where(lane < 64, both[:half], both[half:])
+
+
+def block_kernel(
+    a_hbm, b_hbm, tok_ref, cot_ref, ids_ref,
+    act_ref, ig_ref, ga_hbm, gb_hbm,
+    wa, wb, small, cur, mid, kv, dkv, ids_got, bias, bias_t,
+    normed_s, unit1, scale1, q_s, att_s, unit2, scale2, nm_s, slope_s, actv_s, lse_s,
+    branch_s, hg_s, aog_s, pg_s, qbd, dobd, delta_s, m_s, l_s, acc_s, sums,
+    far_out, near_out, far_in, near_in, stage,
+    wsem, isem, fsend, frecv, bsend, brecv, gsem,
+):
+    chunk, nxt, prv = ring()
+    T = tok_ref.shape[0]
+    D = tok_ref.shape[1]
+    R = cot_ref.shape[0]
+    FF = wb.shape[0]
+    pairs = D // 128
+    S = 3 * T
+    q_cols, kv_cols = pl.ds(0, D), pl.ds(D, 2 * D)
+    out_cols = pl.ds(3 * D, D)
+    up0 = 4 * D
+    small0 = up0 + FF
+
+    barrier = pltpu.get_barrier_semaphore()
+    for peer in (nxt, prv):
+        pl.semaphore_signal(barrier, inc=1, device_id=peer, device_id_type=MESH)
+    parts = (
+        (a_hbm.at[:, pl.ds(small0, 128)], wa.at[:, pl.ds(small0, 128)]),
+        (a_hbm.at[:, pl.ds(0, 3 * D)], wa.at[:, pl.ds(0, 3 * D)]),
+        (a_hbm.at[:, out_cols], wa.at[:, out_cols]),
+        (a_hbm.at[:, pl.ds(up0, FF)], wa.at[:, pl.ds(up0, FF)]),
+        (b_hbm, wb),
     )
-
-
-def merge_heads(tensor):
-    return tensor.reshape(tensor.shape[0], tensor.shape[1], tensor.shape[2] * tensor.shape[3])
-
-
-def stored_keys(kv_store, pass_count, model_width, head_count):
-    joined = jnp.concatenate(kv_store[:pass_count], axis=1)
-    return (
-        split_heads(joined[:, :, :model_width], head_count),
-        split_heads(joined[:, :, model_width:], head_count),
-    )
-
-
-def score_block(queries, key_heads, allowed_now):
-    scores = (
-        jnp.einsum("sqhe,skhe->shqk", queries, key_heads, preferred_element_type=jnp.float32)
-        * 0.125
-    )
-    return jnp.where(allowed_now[:, None], scores, -1e30)
+    fetch = [pltpu.make_async_copy(src, dst, wsem.at[n]) for n, (src, dst) in enumerate(parts)]
+    for copy in fetch:
+        copy.start()
+    pl.semaphore_wait(barrier, 2)
+
+    def remote(src, dst, send_sem, recv_sem, to):
+        return pltpu.make_async_remote_copy(
+            src_ref=src, dst_ref=dst, send_sem=send_sem, recv_sem=recv_sem, device_id=to, device_id_type=MESH
+        )
+
+    first_ids = remote(ids_ref.at[pl.ds(1, 2)], ids_got.at[pl.ds(0, 2)], isem.at[0], isem.at[1], nxt)
+    first_ids.start()
+    cur[...] = tok_ref[...].astype(F32)
+    sums[...] = jnp.zeros_like(sums)
+    fetch[0].wait()
+    small[...] = jnp.transpose(wa[:, pl.ds(small0, 128)].astype(F32))
+
+    @pl.loop(0, R * 3)
+    def _(step):
+        dkv[pl.ds(pl.multiple_of(step * T, T), T), :] = jnp.zeros((T, 2 * D), F32)
+
+    first_ids.wait()
+    second_ids = remote(ids_got.at[1], ids_got.at[2], isem.at[2], isem.at[3], nxt)
+    second_ids.start()
+    second_ids.wait()
+    key_row = ids_ref[0, 0:1, :] + ids_got[0, 0:1, :] + ids_got[2, 0:1, :]
+    own_row = ids_ref[0, 0:1, 0:128] + ids_ref[1, 0:1, 0:128]
+    own_col = jnp.transpose(jnp.broadcast_to(own_row, (128, 128)))[:, 0:1]
+    shape = (2 * T, 4 * T)
+    key = lax.broadcasted_iota(jnp.int32, shape, 1)
+    query = lax.broadcasted_iota(jnp.int32, shape, 0)
+    query = jnp.where(query >= T, query - T, query)
+    slot = key // T
+    allowed = (jnp.broadcast_to(key_row, shape) == jnp.broadcast_to(own_col, shape)) & (slot < 3)
+    allowed = allowed & (slot <= chunk) & ((slot > 0) | (key <= query))
+    full_bias = jnp.where(allowed, 0.0, -1e30).astype(F32)
+    bias[...] = full_bias
+    bias_t[...] = jnp.transpose(full_bias)
+
+    def small_row(index):
+        return small[pl.ds(index, 1), :]
+
+    def rows(r):
+        return pl.ds(pl.multiple_of(r * T, T), T)
+
+    def keys(r, first, count):
+        return pl.ds(pl.multiple_of(r * S + first * T, T), count * T)
+
+    def kv_copies(r):
+        own, near, far = keys(r, 0, 1), keys(r, 1, 1), keys(r, 2, 1)
+        return (
+            remote(kv.at[own], kv.at[near], fsend.at[0, r], frecv.at[0, r], nxt),
+            remote(kv.at[near], kv.at[far], fsend.at[1, r], frecv.at[1, r], nxt),
+        )
+
+    def attend(row_slice, lanes):
+        for p in range(pairs):
+            cols = pl.ds(p * 128, 128)
+            state = pl.ds(p * 128, 128)
+            values = pl.ds(D + p * 128, 128)
+            scores = mm_nt(qbd[state, :], kv[row_slice, cols]) + bias[:, lanes]
+            old = m_s[state, :]
+            new = jnp.maximum(old, jnp.max(scores, axis=-1, keepdims=True))
+            weight = jnp.exp(scores - new[:, 0:1])
+            shrink = jnp.exp(old - new)
+            m_s[state, :] = new
+            l_s[state, :] = l_s[state, :] * shrink + jnp.sum(weight, axis=-1, keepdims=True)
+            acc_s[state, :] = acc_s[state, :] * shrink + mm(weight.astype(BF16), kv[row_slice, values])
+
+    def forward(r, carry):
+        mine = rows(r)
+        first, second = kv_copies(r)
+        entry = cur[...] + small_row(4 + r)
+        unit, scale = norm_forward(entry)
+        unit1[mine, :] = unit
+        scale1[mine, :] = jnp.broadcast_to(scale, (T, 128))
+        normed = (unit * small_row(0) + small_row(1)).astype(BF16)
+        normed_s[mine, :] = normed
+
+        @pl.when(r == 0)
+        def _():
+            fetch[1].wait()
+
+        kv[keys(r, 0, 1), :] = mm(normed, wa[:, kv_cols]).astype(BF16)
+        first.start()
+        queries = mm(normed, wa[:, q_cols]).astype(BF16) * jnp.asarray(0.125, BF16)
+        q_s[mine, :] = queries
+        for p in range(pairs):
+            qbd[pl.ds(p * 128, 128), :] = split_pair(queries[:, p * 128 : p * 128 + 128])
+        m_s[...] = jnp.full_like(m_s, -1e30)
+        l_s[...] = jnp.zeros_like(l_s)
+        acc_s[...] = jnp.zeros_like(acc_s)
+        lax.fori_loop(0, r, lambda e, c: (attend(keys(e, 0, 3), pl.ds(0, S)), c)[1], 0)
+        attend(keys(r, 0, 1), pl.ds(0, T))
+        first.wait_recv()
+        second.start()
+        attend(keys(r, 1, 1), pl.ds(T, T))
+        second.wait_recv()
+        attend(keys(r, 2, 1), pl.ds(2 * T, T))
+        for p in range(pairs):
+            state = pl.ds(p * 128, 128)
+            total = l_s[state, :]
+            att_s[mine, pl.ds(p * 128, 128)] = join_pair(acc_s[state, :] / total).astype(BF16)
+            lse_s[pl.ds(pl.multiple_of(r * 8, 8), 8), pl.ds(p * 128, 128)] = jnp.transpose(
+                m_s[state, :] + jnp.log(total)
+            )[0:8, :]
+
+        @pl.when(r == 0)
+        def _():
+            fetch[2].wait()
+
+        middle = entry + mm(att_s[mine, :], wa[:, out_cols])
+        unit, scale = norm_forward(middle)
+        unit2[mine, :] = unit
+        scale2[mine, :] = jnp.broadcast_to(scale, (T, 128))
+        normed = (unit * small_row(2) + small_row(3)).astype(BF16)
+        nm_s[mine, :] = normed
+
+        @pl.when(r == 0)
+        def _():
+            fetch[3].wait()
+            fetch[4].wait()
+
+        total = middle
+        for j in range(FF // D):
+            hidden = mm(normed, wa[:, pl.ds(up0 + j * D, D)])
+            square = hidden * hidden
+            root = 0.7978845608028654
+            t = jnp.tanh(root * hidden * (1.0 + 0.044715 * square))
+            slope_s[mine, pl.ds(j * D, D)] = 0.5 * (1.0 + t) + 0.5 * root * hidden * (1.0 - t * t) * (
+                1.0 + 3 * 0.044715 * square
+            )
+            activated = (0.5 * hidden * (1.0 + t)).astype(BF16)
+            actv_s[mine, pl.ds(j * D, D)] = activated
+            total = total + mm(activated, wb[pl.ds(j * D, D), :])
+        cur[...] = total
+        act_ref[r] = total.astype(BF16)
+        first.wait_send()
+        second.wait_send()
+        return carry
+
+    lax.fori_loop(0, R, forward, 0)
+    cur[...] = jnp.zeros_like(cur)
+
+    def grad_block(e):
+        block = keys(e, 0, 3)
+        for p in range(pairs):
+            cols = pl.ds(p * 128, 128)
+            state = pl.ds(p * 128, 128)
+            values = pl.ds(D + p * 128, 128)
+            k_pair, v_pair = kv[block, cols], kv[block, values]
+            q_pair, o_pair = qbd[state, :], dobd[state, :]
+            scores = mm_nt(k_pair, q_pair) + bias_t[0:S, :]
+            probs = jnp.exp(scores - delta_s[0:1, cols])
+            grad = probs * (mm_nt(v_pair, o_pair) - delta_s[8:9, cols])
+            low = grad.astype(BF16)
+            dkv[block, cols] += mm(low, q_pair)
+            dkv[block, values] += mm(probs.astype(BF16), o_pair)
+            acc_s[state, :] += mm_tn(low, k_pair)
+
+    def backward(i, carry):
+        r = R - 1 - i
+        mine = rows(r)
+        grad_out = cot_ref[r].astype(F32) + cur[...]
+        branch = grad_out.astype(BF16)
+        branch_s[mine, :] = branch
+        e = jnp.zeros((T, D), F32)
+        for j in range(FF // D):
+            part = pl.ds(j * D, D)
+            low = (mm_nt(branch, wb[part, :]) * slope_s[mine, part]).astype(BF16)
+            hg_s[mine, part] = low
+            e = e + mm_nt(low, wa[:, pl.ds(up0 + j * D, D)])
+        unit = unit2[mine, :]
+        sums[2:3, :] += jnp.sum(e * unit, axis=0, keepdims=True)
+        sums[3:4, :] += jnp.sum(e, axis=0, keepdims=True)
+        middle_grad = grad_out + norm_backward(e, small_row(2), unit, scale2[mine, 0:1])
+        mid[...] = middle_grad
+        low = middle_grad.astype(BF16)
+        aog_s[mine, :] = low
+        mixed = mm_nt(low, wa[:, out_cols]).astype(BF16)
+        queries = q_s[mine, :]
+        attended = att_s[mine, :]
+        for p in range(pairs):
+            state = pl.ds(p * 128, 128)
+            lo, hi = p * 128, p * 128 + 128
+            qbd[state, :] = split_pair(queries[:, lo:hi])
+            o_pair = split_pair(mixed[:, lo:hi])
+            dobd[state, :] = o_pair
+            twice = jnp.concatenate([attended[:, lo:hi], attended[:, lo:hi]], axis=0)
+            product = jnp.transpose(o_pair.astype(F32) * twice.astype(F32))
+            delta_s[8:16, lo:hi] = jnp.broadcast_to(jnp.sum(product, axis=0, keepdims=True), (8, 128))
+        delta_s[0:8, :] = lse_s[pl.ds(pl.multiple_of(r * 8, 8), 8), :]
+        acc_s[...] = jnp.zeros_like(acc_s)
+        grad_block(r)
+        far_out[r] = dkv[keys(r, 2, 1), :].astype(BF16)
+        far = remote(far_out.at[r], far_in.at[r], bsend.at[0, r], brecv.at[0, r], prv)
+        far.start()
+        lax.fori_loop(0, r, lambda e, c: (grad_block(e), c)[1], 0)
+        far.wait_recv()
+        near_out[r] = (dkv[keys(r, 1, 1), :] + far_in[r].astype(F32)).astype(BF16)
+        near = remote(near_out.at[r], near_in.at[r], bsend.at[1, r], brecv.at[1, r], prv)
+        near.start()
+        for p in range(pairs):
+            pg_s[mine, pl.ds(p * 128, 128)] = (0.125 * join_pair(acc_s[pl.ds(p * 128, 128), :])).astype(BF16)
+        e = mm_nt(pg_s[mine, q_cols], wa[:, q_cols])
+        near.wait_recv()
+        low = (dkv[keys(r, 0, 1), :] + near_in[r].astype(F32)).astype(BF16)
+        pg_s[mine, kv_cols] = low
+        e = e + mm_nt(low, wa[:, kv_cols])
+        unit = unit1[mine, :]
+        sums[0:1, :] += jnp.sum(e * unit, axis=0, keepdims=True)
+        sums[1:2, :] += jnp.sum(e, axis=0, keepdims=True)
+        entry_grad = mid[...] + norm_backward(e, small_row(0), unit, scale1[mine, 0:1])
+        cur[...] = entry_grad
+        sums[pl.ds(4 + r, 1), :] = jnp.sum(entry_grad, axis=0, keepdims=True)
+        far.wait_send()
+        near.wait_send()
+        return carry
+
+    lax.fori_loop(0, R, backward, 0)
+    ig_ref[...] = cur[...]
+
+    wa[:, pl.ds(small0, 128)] = jnp.transpose(sums[...]).astype(BF16)
+    tail = pltpu.make_async_copy(wa.at[:, pl.ds(small0, 128)], ga_hbm.at[:, pl.ds(small0, 128)], wsem.at[0])
+    tail.start()
+
+    def piece(n, features, grads, target):
+        hold = n % 2 if isinstance(n, int) else lax.rem(n, 2)
+        copy = pltpu.make_async_copy(stage.at[hold], target, gsem.at[hold])
+        if not (isinstance(n, int) and n < 2):
+            @pl.when(n >= 2)
+            def _():
+                copy.wait()
+
+        stage[hold] = mm_tn(features, grads).astype(BF16)
+        copy.start()
+
+    def wide(n0, count, feature_ref, grad_ref, col0):
+        def body(j, c):
+            part = pl.ds(pl.multiple_of(j * D, D), D)
+            piece(n0 + j, feature_ref[...], grad_ref[:, part], ga_hbm.at[:, pl.ds(pl.multiple_of(col0 + j * D, D), D)])
+            return c
+
+        lax.fori_loop(0, count, body, 0)
+
+    wide(0, 3, normed_s, pg_s, 0)
+    wide(3, 1, att_s, aog_s, 3 * D)
+    wide(4, FF // D, nm_s, hg_s, up0)
+
+    def tall(j, c):
+        part = pl.ds(pl.multiple_of(j * D, D), D)
+        piece(4 + FF // D + j, actv_s[:, part], branch_s[...], gb_hbm.at[part, :])
+        return c
+
+    lax.fori_loop(0, FF // D, tall, 0)
+    for hold in (0, 1):
+        pltpu.make_async_copy(stage.at[hold], gb_hbm.at[pl.ds(0, D), :], gsem.at[hold]).wait()
+    tail.wait()
+
+
+def run_block(all_a, all_b, tokens, cot, ids):
+    T, D = tokens.shape
+    R = cot.shape[0]
+    FF = all_b.shape[0]
+    rows = R * T
+    V = pltpu.VMEM
+    DMA = pltpu.SemaphoreType.DMA
+    return pl.pallas_call(
+        block_kernel,
+        out_shape=(
+            jax.ShapeDtypeStruct((R, T, D), BF16),
+            jax.ShapeDtypeStruct((T, D), F32),
+            jax.ShapeDtypeStruct(all_a.shape, BF16),
+            jax.ShapeDtypeStruct(all_b.shape, BF16),
+        ),
+        in_specs=[pl.BlockSpec(memory_space=pl.ANY)] * 2 + [pl.BlockSpec(memory_space=pltpu.VMEM)] * 3,
+        out_specs=[pl.BlockSpec(memory_space=pltpu.VMEM)] * 2 + [pl.BlockSpec(memory_space=pl.ANY)] * 2,
+        scratch_shapes=[
+            V(all_a.shape, BF16), V(all_b.shape, BF16), V((128, D), F32), V((T, D), F32), V((T, D), F32),
+            V((3 * rows, 2 * D), BF16), V((3 * rows, 2 * D), F32), V((3, 8, 256), F32),
+            V((128, 256), F32), V((256, 128), F32),
+            V((rows, D), BF16), V((rows, D), F32), V((rows, 128), F32), V((rows, D), BF16), V((rows, D), BF16),
+            V((rows, D), F32), V((rows, 128), F32), V((rows, D), BF16), V((rows, FF), F32), V((rows, FF), BF16),
+            V((8 * R, D), F32),
+            V((rows, D), BF16), V((rows, FF), BF16), V((rows, D), BF16), V((rows, 3 * D), BF16),
+            V((D, 128), BF16), V((D, 128), BF16), V((16, D), F32), V((D, 128), F32), V((D, 128), F32), V((D, 128), F32),
+            V((128, D), F32),
+            V((R, T, 2 * D), BF16), V((R, T, 2 * D), BF16), V((R, T, 2 * D), BF16), V((R, T, 2 * D), BF16),
+            V((2, D, D), BF16),
+            DMA((5,)), DMA((4,)), DMA((2, R)), DMA((2, R)), DMA((2, R)), DMA((2, R)), DMA((2,)),
+        ],
+        compiler_params=pltpu.CompilerParams(
+            collective_id=2, has_side_effects=True, vmem_limit_bytes=VMEM_LIMIT
+        ),
+    )(all_a, all_b, tokens, cot, ids)
 
 
 def on_device(
@@ -328,174 +651,38 @@
     segment_ids,
     cotangent,
 ):
-    seq_count, local_tok, model_width = tokens.shape
+    _, local_tok, model_width = tokens.shape
     repeats = pass_embed.shape[0]
-    head_count = H
-    full_tok = local_tok * lax.axis_size("ctx")
-    all_ids = lax.all_gather(segment_ids, "ctx", axis=1, tiled=True)
-    query_pos = lax.axis_index("ctx") * local_tok + jnp.arange(local_tok, dtype=jnp.int32)
-    key_pos = jnp.arange(full_tok, dtype=jnp.int32)
-    allowed = (segment_ids[:, :, None] == all_ids[:, None, :]) & (
-        key_pos[None, None, :] <= query_pos[None, :, None]
-    )
-    current = tokens.astype(jnp.float32)
-    log_totals = []
-    kv_store = []
-    pass_outputs = []
-    normed_keep = []
-    query_keep = []
-    attended_keep = []
-    normed_mid_keep = []
-    activated_keep = []
-    first_backs = []
-    second_backs = []
-    gelu_backs = []
+    qkv_cols, ff_width = qkv_weight.shape[1], up_weight.shape[1]
     small_in = jnp.stack([attn_gain, attn_shift, ffn_gain, ffn_shift], axis=1)
     small_in = jnp.concatenate([small_in, pass_embed.T], axis=1)
     small_in = jnp.pad(small_in, ((0, 0), (0, 128 - small_in.shape[1])))
     rows_a = jnp.concatenate([qkv_weight, out_weight, up_weight, small_in], axis=1)
-    if (lax.axis_size("dp"), lax.axis_size("ctx")) == (8, 4):
+    block_of_slice = (lax.axis_size("dp"), lax.axis_size("ctx")) == (8, 4)
+    if block_of_slice:
         all_a, all_b = gather_blocks(rows_a, down_weight)
     else:
         all_a = lax.all_gather(rows_a, ("dp", "ctx"), axis=0)
         all_b = lax.all_gather(down_weight, ("dp", "ctx"), axis=0)
     all_a = all_a.reshape(model_width, -1)
-    down_full = all_b.reshape(-1, model_width)
-    qkv_cols, ff_width = qkv_weight.shape[1], up_weight.shape[1]
-    qkv_full = all_a[:, :qkv_cols]
-    out_full = all_a[:, qkv_cols : qkv_cols + model_width]
-    up_full = all_a[:, qkv_cols + model_width : qkv_cols + model_width + ff_width]
-    small_rows = all_a[:, qkv_cols + model_width + ff_width :].T
-    gain_first, shift_first, gain_second, shift_second = (small_rows[row] for row in range(4))
-    embed_full = small_rows[4 : 4 + repeats]
-    for repeat in range(repeats):
-        entry = current + embed_full[repeat].astype(jnp.float32)
-        normed, norm_first_back = jax.vjp(
-            layer_norm, entry, gain_first.astype(jnp.float32), shift_first.astype(jnp.float32)
-        )
-        normed_lo = normed.astype(jnp.bfloat16)
-        projected = project(normed_lo, qkv_full).astype(jnp.bfloat16)
-        local_kv = projected[:, :, model_width:]
-        kv_store.append(lax.all_gather(local_kv, "ctx", axis=1, tiled=True))
-        key_heads, value_heads = stored_keys(kv_store, repeat + 1, model_width, head_count)
-        queries = split_heads(projected[:, :, :model_width], head_count)
-        allowed_now = jnp.tile(allowed, (1, 1, repeat + 1))
-        scores = score_block(queries, key_heads, allowed_now)
-        row_max = jnp.max(scores, axis=-1, keepdims=True)
-        shifted = jnp.exp(scores - row_max)
-        total_exp = jnp.sum(shifted, axis=-1, keepdims=True)
-        log_totals.append(row_max + jnp.log(total_exp))
-        probs_lo = (shifted / total_exp).astype(jnp.bfloat16)
-        attended = merge_heads(
-            jnp.einsum("shqk,skhe->sqhe", probs_lo, value_heads, preferred_element_type=jnp.float32)
-        ).astype(jnp.bfloat16)
-        middle = entry + project(attended, out_full)
-        normed_mid, norm_second_back = jax.vjp(
-            layer_norm, middle, gain_second.astype(jnp.float32), shift_second.astype(jnp.float32)
-        )
-        normed_mid_lo = normed_mid.astype(jnp.bfloat16)
-        activated, gelu_back = jax.vjp(gelu_tanh, project(normed_mid_lo, up_full))
-        activated_lo = activated.astype(jnp.bfloat16)
-        current = middle + project(activated_lo, down_full)
-        pass_outputs.append(current.astype(jnp.bfloat16))
-        normed_keep.append(normed_lo)
-        query_keep.append(queries)
-        attended_keep.append(attended)
-        normed_mid_keep.append(normed_mid_lo)
-        activated_keep.append(activated_lo)
-        first_backs.append(norm_first_back)
-        second_backs.append(norm_second_back)
-        gelu_backs.append(gelu_back)
-    small_totals = [jnp.zeros((model_width,), jnp.float32) for slot in range(4)]
-    key_grads = [
-        jnp.zeros((seq_count, full_tok, 2 * model_width), jnp.float32) for earlier in range(repeats)
-    ]
-    branch_keep = [None] * repeats
-    hidden_keep = [None] * repeats
-    attn_out_keep = [None] * repeats
-    proj_keep = [None] * repeats
-    embed_rows = [None] * repeats
-    carry = jnp.zeros((seq_count, local_tok, model_width), jnp.float32)
-    cot_split = cotangent.reshape(seq_count, local_tok, repeats, model_width)
-    for repeat in reversed(range(repeats)):
-        grad_out = cot_split[:, :, repeat].astype(jnp.float32) + carry
-        queries = query_keep[repeat]
-        key_heads, value_heads = stored_keys(kv_store, repeat + 1, model_width, head_count)
-        allowed_now = jnp.tile(allowed, (1, 1, repeat + 1))
-        attn_probs = jnp.exp(score_block(queries, key_heads, allowed_now) - log_totals[repeat])
-        probs_lo = attn_probs.astype(jnp.bfloat16)
-        branch_grad = grad_out.astype(jnp.bfloat16)
-        branch_keep[repeat] = branch_grad
-        hidden_grad = gelu_backs[repeat](project_back(branch_grad, down_full))[0].astype(
-            jnp.bfloat16
-        )
-        hidden_keep[repeat] = hidden_grad
-        middle_grad, gain_second_grad, shift_second_grad = second_backs[repeat](
-            project_back(hidden_grad, up_full)
-        )
-        small_totals[2] = small_totals[2] + gain_second_grad
-        small_totals[3] = small_totals[3] + shift_second_grad
-        middle_grad = middle_grad + grad_out
-        attn_out_grad = middle_grad.astype(jnp.bfloat16)
-        attn_out_keep[repeat] = attn_out_grad
-        mixed_grad = split_heads(
-            project_back(attn_out_grad, out_full).astype(jnp.bfloat16), head_count
-        )
-        prob_grad = jnp.einsum(
-            "sqhe,skhe->shqk", mixed_grad, value_heads, preferred_element_type=jnp.float32
-        )
-        score_grad = (
-            attn_probs * (prob_grad - jnp.sum(prob_grad * attn_probs, axis=-1, keepdims=True))
-        ).astype(jnp.bfloat16)
-        query_grad = (
-            jnp.einsum("shqk,skhe->sqhe", score_grad, key_heads, preferred_element_type=jnp.float32)
-            * 0.125
-        )
-        key_grad = (
-            jnp.einsum("shqk,sqhe->skhe", score_grad, queries, preferred_element_type=jnp.float32)
-            * 0.125
-        )
-        value_grad = jnp.einsum(
-            "shqk,sqhe->skhe", probs_lo, mixed_grad, preferred_element_type=jnp.float32
-        )
-        joined_grad = jnp.concatenate([merge_heads(key_grad), merge_heads(value_grad)], axis=-1)
-        for earlier in range(repeat + 1):
-            key_grads[earlier] = (
-                key_grads[earlier] + joined_grad[:, earlier * full_tok : (earlier + 1) * full_tok]
-            )
-        pass_grads = key_grads[repeat]
-        own_grad = lax.psum_scatter(
-            pass_grads.astype(jnp.bfloat16), "ctx", scatter_dimension=1, tiled=True
-        ).astype(jnp.float32)
-        proj_grad = jnp.concatenate([merge_heads(query_grad), own_grad], axis=-1).astype(
-            jnp.bfloat16
-        )
-        proj_keep[repeat] = proj_grad
-        entry_grad, gain_first_grad, shift_first_grad = first_backs[repeat](
-            project_back(proj_grad, qkv_full)
-        )
-        small_totals[0] = small_totals[0] + gain_first_grad
-        small_totals[1] = small_totals[1] + shift_first_grad
-        carry = entry_grad + middle_grad
-        embed_rows[repeat] = jnp.sum(carry, axis=(0, 1))
-    qkv_total = outer_sum(normed_keep, proj_keep)
-    out_total = outer_sum(attended_keep, attn_out_keep)
-    up_total = outer_sum(normed_mid_keep, hidden_keep)
-    down_total = outer_sum(activated_keep, branch_keep)
-    embed_grad = jnp.stack(embed_rows, axis=0)
-    small_total = jnp.concatenate([jnp.stack(small_totals, axis=0), embed_grad], axis=0).T
-    small_total = jnp.pad(small_total, ((0, 0), (0, 128 - small_total.shape[1])))
-    grad_a = jnp.concatenate(
-        [qkv_total.astype(jnp.bfloat16), out_total.astype(jnp.bfloat16), up_total.astype(jnp.bfloat16), small_total.astype(jnp.bfloat16)], axis=1
-    ).reshape(-1, *rows_a.shape)
-    grad_b = down_total.astype(jnp.bfloat16).reshape(-1, *down_weight.shape)
-    if (lax.axis_size("dp"), lax.axis_size("ctx")) == (8, 4):
+    all_b = all_b.reshape(-1, model_width)
+    own_ids = segment_ids.astype(F32)
+    ids = jnp.stack([jnp.pad(own_ids, ((0, 0), (s * local_tok, (3 - s) * local_tok))) for s in range(3)])
+    ids = jnp.broadcast_to(ids, (3, 8, 4 * local_tok))
+    cot = cotangent.reshape(local_tok, repeats, model_width).transpose(1, 0, 2)
+    outputs, input_grad, grad_a, grad_b = run_block(all_a, all_b, tokens[0], cot, ids)
+    grad_a = grad_a.reshape(-1, *rows_a.shape)
+    grad_b = grad_b.reshape(-1, *down_weight.shape)
+    if block_of_slice:
         own_a, own_b = reduce_blocks(grad_a, grad_b)
     else:
-        own_a = lax.psum_scatter(grad_a.astype(jnp.float32), ("dp", "ctx"), scatter_dimension=0)
-        own_b = lax.psum_scatter(grad_b.astype(jnp.float32), ("dp", "ctx"), scatter_dimension=0)
+        own_a = lax.psum_scatter(grad_a.astype(F32), ("dp", "ctx"), scatter_dimension=0)
+        own_b = lax.psum_scatter(grad_b.astype(F32), ("dp", "ctx"), scatter_dimension=0)
     own_small = own_a[:, qkv_cols + model_width + ff_width :].T
-    reduced = (
+    activations = outputs.transpose(1, 0, 2).reshape(1, local_tok * repeats, model_width)
+    return (
+        activations,
+        input_grad[None],
         own_a[:, :qkv_cols],
         own_a[:, qkv_cols : qkv_cols + model_width],
         own_a[:, qkv_cols + model_width : qkv_cols + model_width + ff_width],
@@ -505,22 +692,6 @@
         own_small[2],
         own_small[3],
         own_small[4 : 4 + repeats],
-    )
-    activations = jnp.stack(pass_outputs, axis=2).reshape(
-        seq_count, local_tok * repeats, model_width
-    )
-    return (
-        activations,
-        carry,
-        reduced[0],
-        reduced[1],
-        reduced[2],
-        reduced[3],
-        reduced[4],
-        reduced[5],
-        reduced[6],
-        reduced[7],
-        reduced[8],
     )
 
 

time: 763 us -> 369 us (0.48); the launches traced: 753 us -> 369 us
  Pallas kernels: 148 us -> 347 us
  local copies, waits for them, and re-layouts: 192 us -> 18.4 us
  matrix products: 173 us -> 0 us
  blocking collectives: 101 us -> 0 us
  other arithmetic: 82.3 us -> 2.39 us
  waiting for transfers between devices: 36.9 us -> 0 us
  between operations: 18 us -> 0.7 us
    pallas_call x0 -> x1, Pallas kernels: none -> 198 us  [run_block(): pl.pallas_call(block_kernel, out_shape=(jax.ShapeDtypeStruct((R, T, D), B...]
    dot_general x74 -> x0, matrix products: 173 us -> none  [the longest x20 70.6 us: project_back(): jnp.einsum('ste,de->std', features, matrix, preferred_element_type=jnp.fl...]
    unnamed x544 -> x6, local copies, waits for them, and re-layouts: 106 us -> 3.82 us
    all_gather x5 -> x0, blocking collectives: 84.5 us -> none  [on_device(): kv_store.append(lax.all_gather(local_kv, 'ctx', axis=1, tiled=True))]
    slice x27 -> x0, local copies, waits for them, and re-layouts: 38.9 us -> none  [the longest x10 20.4 us: stored_keys(): joined[:, :, :model_width]]
    unnamed x10 -> x0, waiting for transfers between devices: 36.9 us -> none
    reduce_sum x45 -> x0, other arithmetic: 25.9 us -> none  [the longest x11 12.4 us: layer_norm(): return centered * lax.rsqrt(variance + 1e-05) * gain_row + shift_row]
    another operation x20 -> x1, local copies, waits for them, and re-layouts: 19.3 us -> 0.08 us  [on_device(): jnp.stack([jnp.pad(own_ids, ((0, 0), (s * local_tok, (3 - s) * local_tok)...]
  transfers between devices with their start and end apart: 5 -> 0, of which waited for: 4 -> 0; matrix products, arithmetic and copies ran while one was open for 10% -> 0% of each run, Pallas kernels for 0% -> 0%
where the time goes in v2:
time: 369 us
  Pallas kernels  347 us (94%)
  local copies, waits for them, and re-layouts  18.4 us (5%)
    pallas_call x1, Pallas kernels, run_block(): pl.pallas_call(block_kernel, out_shape=(jax.ShapeDtypeStruct((R, T, D), B...  198 us
    pallas_call x1, Pallas kernels, gather_blocks(): pl.pallas_call(gather_kernel, out_shape=(jax.ShapeDtypeStruct((count,) +...  74.6 us
    pallas_call x1, Pallas kernels, reduce_blocks(): pl.pallas_call(reduce_kernel, out_shape=(jax.ShapeDtypeStruct((ra, ca), F...  74.6 us

profile of v2, /device:TPU:0, one launch (start us, length us, event | category | flops | bytes accessed | tf_op | source)
XLA Modules:
  0.0 368.8 jit_solution(9653124007243158158)
XLA Ops:
  0.6 0.7 convert_element_type.11
  1.3 0.1 pad_bitcast_fusion.2
  1.4 0.7 copy.30
  2.1 0.7 copy.31
  2.9 0.7 copy.32
  3.6 0.7 copy.33
  4.4 0.8 copy.29
  5.2 0.1 concatenate.6
  5.2 0.6 broadcast_in_dim.11.ids_ref
  5.9 1.7 fusion.1.a_ref
  7.6 1.3 reshape.42
  8.8 0.9 copy.38
  9.7 74.6 %shard_map.203 = (bf16[32,24,6272]{2,1,0:T(8,128)(2,1)}, bf16[32,96,768]{2,1,0:T(8,128)(2,1)}) custom-call(bf16[24,6272]{1,0:T(8,128)(2,1)} %fusion.1.a_ref, bf16[96,768]{1,0:T(8,128)(2,1)} %b_ref.1), custom_call_target="tpu_custom_call" | custom-call | tf_op jit(solution)/shard_map/pallas_call | solution.py:121
  84.4 198.1 %shard_map.204 = (bf16[5,64,768]{2,1,0:T(8,128)(2,1)}, f32[64,768]{1,0:T(8,128)}, bf16[768,6272]{1,0:T(8,128)(2,1)}, bf16[3072,768]{1,0:T(8,128)(2,1)}) custom-call(bf16[768,6272]{1,0:T(8,128)(2,1)} %bitcast.26, bf16[3072,768]{1,0:T(8,128)(2,1)} %bitcast.28, bf16[64,768]{1,0:T(8,128)(2,1)} %bitcast.32, bf16[5,64,768]{2,1,0:T(8,128)(2,1)} %bitcast.29, ...), custom_call_target="tpu_custom_call" | custom-call | tf_op jit(solution)/shard_map/pallas_call | solution.py:610
  282.5 0.0 copy-start
  282.5 1.4 copy.35
  283.8 1.0 reshape.43
  284.8 74.6 %shard_map.205 = (f32[24,6272]{1,0:T(8,128)}, f32[96,768]{1,0:T(8,128)}) custom-call(bf16[32,24,6272]{2,1,0:T(8,128)(2,1)} %bitcast.25, bf16[32,96,768]{2,1,0:T(8,128)(2,1)} %bitcast.27), custom_call_target="tpu_custom_call" | custom-call | tf_op jit(solution)/shard_map/pallas_call | solution.py:243
  359.4 0.7 slice_bitcast_fusion
  360.1 0.7 slice_reduce_fusion
  360.9 0.1 slice.40
  360.9 0.7 copy.36
  361.6 1.5 slice.28
  363.1 1.6 slice.27
  364.8 1.7 slice.29
  366.5 0.0 copy-done
  366.5 0.7 copy.41
  367.1 1.7 copy.42
  (1 shorter events, 0.0 us)
Async XLA Ops:
  282.5 84.0 %copy-start = (f32[64,768]{1,0:T(8,128)S(1)}, f32[64,768]{1,0:T(8,128)}, u32[]{:S(2)}) copy-start(f32[64,768]{1,0:T(8,128)} %get-tuple-element.22) | copy-start | bytes 589828

commit v3 on v2

--- a/solution.py
+++ b/solution.py
@@ -266,8 +266,20 @@
 def ring():
     dp = lax.axis_index("dp")
     z = lax.axis_index("ctx")
-    size = lax.axis_size("ctx")
-    return z, (dp, lax.rem(z + 1, size)), (dp, lax.rem(z + size - 1, size))
+    core = lax.rem(dp, 2)
+    odd = lax.rem(z, 2)
+    other = dp + 1 - 2 * core
+    across = 1 - 2 * odd
+    return 2 * odd + core, (other, z + core * across), (other, z + (1 - core) * across)
+
+
+def regroup(count_dp):
+    moves = []
+    for dp in range(count_dp):
+        for c in range(4):
+            to = (dp - dp % 2 + c % 2) * 4 + 2 * (dp % 2) + c // 2
+            moves.append((dp * 4 + c, to))
+    return moves
 
 
 def mm(x, w):
@@ -312,7 +324,7 @@
 def block_kernel(
     a_hbm, b_hbm, tok_ref, cot_ref, ids_ref,
     act_ref, ig_ref, ga_hbm, gb_hbm,
-    wa, wb, small, cur, mid, kv, dkv, ids_got, bias, bias_t,
+    wa, wb, small, cur, mid, kv, dkv, ids_got, bias_t,
     normed_s, unit1, scale1, q_s, att_s, unit2, scale2, nm_s, slope_s, actv_s, lse_s,
     branch_s, hg_s, aog_s, pg_s, qbd, dobd, delta_s, m_s, l_s, acc_s, sums,
     far_out, near_out, far_in, near_in, stage,
@@ -376,7 +388,6 @@
     allowed = (jnp.broadcast_to(key_row, shape) == jnp.broadcast_to(own_col, shape)) & (slot < 3)
     allowed = allowed & (slot <= chunk) & ((slot > 0) | (key <= query))
     full_bias = jnp.where(allowed, 0.0, -1e30).astype(F32)
-    bias[...] = full_bias
     bias_t[...] = jnp.transpose(full_bias)
 
     def small_row(index):
@@ -395,19 +406,18 @@
             remote(kv.at[near], kv.at[far], fsend.at[1, r], frecv.at[1, r], nxt),
         )
 
-    def attend(row_slice, lanes):
+    def attend(row_slice, slots):
         for p in range(pairs):
             cols = pl.ds(p * 128, 128)
-            state = pl.ds(p * 128, 128)
             values = pl.ds(D + p * 128, 128)
-            scores = mm_nt(qbd[state, :], kv[row_slice, cols]) + bias[:, lanes]
-            old = m_s[state, :]
-            new = jnp.maximum(old, jnp.max(scores, axis=-1, keepdims=True))
-            weight = jnp.exp(scores - new[:, 0:1])
+            scores = mm_nt(kv[row_slice, cols], qbd[cols, :]) + bias_t[slots, :]
+            old = m_s[0:1, cols]
+            new = jnp.maximum(old, jnp.max(scores, axis=0, keepdims=True))
+            weight = jnp.exp(scores - new)
             shrink = jnp.exp(old - new)
-            m_s[state, :] = new
-            l_s[state, :] = l_s[state, :] * shrink + jnp.sum(weight, axis=-1, keepdims=True)
-            acc_s[state, :] = acc_s[state, :] * shrink + mm(weight.astype(BF16), kv[row_slice, values])
+            m_s[0:1, cols] = new
+            l_s[0:1, cols] = l_s[0:1, cols] * shrink + jnp.sum(weight, axis=0, keepdims=True)
+            acc_s[cols, :] = acc_s[cols, :] * shrink + mm_tn(kv[row_slice, values], weight.astype(BF16))
 
     def forward(r, carry):
         mine = rows(r)
@@ -440,12 +450,9 @@
         second.wait_recv()
         attend(keys(r, 2, 1), pl.ds(2 * T, T))
         for p in range(pairs):
-            state = pl.ds(p * 128, 128)
-            total = l_s[state, :]
-            att_s[mine, pl.ds(p * 128, 128)] = join_pair(acc_s[state, :] / total).astype(BF16)
-            lse_s[pl.ds(pl.multiple_of(r * 8, 8), 8), pl.ds(p * 128, 128)] = jnp.transpose(
-                m_s[state, :] + jnp.log(total)
-            )[0:8, :]
+            cols = pl.ds(p * 128, 128)
+            att_s[mine, cols] = join_pair(jnp.transpose(acc_s[cols, :] / l_s[0:1, cols])).astype(BF16)
+        lse_s[pl.ds(pl.multiple_of(r * 8, 8), 8), :] = jnp.broadcast_to(m_s[0:1, :] + jnp.log(l_s[0:1, :]), (8, D))
 
         @pl.when(r == 0)
         def _():
@@ -620,12 +627,12 @@
         scratch_shapes=[
             V(all_a.shape, BF16), V(all_b.shape, BF16), V((128, D), F32), V((T, D), F32), V((T, D), F32),
             V((3 * rows, 2 * D), BF16), V((3 * rows, 2 * D), F32), V((3, 8, 256), F32),
-            V((128, 256), F32), V((256, 128), F32),
+            V((256, 128), F32),
             V((rows, D), BF16), V((rows, D), F32), V((rows, 128), F32), V((rows, D), BF16), V((rows, D), BF16),
             V((rows, D), F32), V((rows, 128), F32), V((rows, D), BF16), V((rows, FF), F32), V((rows, FF), BF16),
             V((8 * R, D), F32),
             V((rows, D), BF16), V((rows, FF), BF16), V((rows, D), BF16), V((rows, 3 * D), BF16),
-            V((D, 128), BF16), V((D, 128), BF16), V((16, D), F32), V((D, 128), F32), V((D, 128), F32), V((D, 128), F32),
+            V((D, 128), BF16), V((D, 128), BF16), V((16, D), F32), V((8, D), F32), V((8, D), F32), V((D, 128), F32),
             V((128, D), F32),
             V((R, T, 2 * D), BF16), V((R, T, 2 * D), BF16), V((R, T, 2 * D), BF16), V((R, T, 2 * D), BF16),
             V((2, D, D), BF16),
@@ -666,7 +673,12 @@
         all_b = lax.all_gather(down_weight, ("dp", "ctx"), axis=0)
     all_a = all_a.reshape(model_width, -1)
     all_b = all_b.reshape(-1, model_width)
-    own_ids = segment_ids.astype(F32)
+    moves = regroup(lax.axis_size("dp"))
+    back = [(to, came) for came, to in moves]
+    axes = ("dp", "ctx")
+    own_ids = lax.ppermute(segment_ids, axes, moves).astype(F32)
+    tokens = lax.ppermute(tokens, axes, moves)
+    cotangent = lax.ppermute(cotangent, axes, moves)
     ids = jnp.stack([jnp.pad(own_ids, ((0, 0), (s * local_tok, (3 - s) * local_tok))) for s in range(3)])
     ids = jnp.broadcast_to(ids, (3, 8, 4 * local_tok))
     cot = cotangent.reshape(local_tok, repeats, model_width).transpose(1, 0, 2)
@@ -679,6 +691,8 @@
         own_a = lax.psum_scatter(grad_a.astype(F32), ("dp", "ctx"), scatter_dimension=0)
         own_b = lax.psum_scatter(grad_b.astype(F32), ("dp", "ctx"), scatter_dimension=0)
     own_small = own_a[:, qkv_cols + model_width + ff_width :].T
+    outputs = lax.ppermute(outputs, axes, back)
+    input_grad = lax.ppermute(input_grad, axes, back)
     activations = outputs.transpose(1, 0, 2).reshape(1, local_tok * repeats, model_width)
     return (
         activations,

time: 369 us -> 346 us (0.938)
  Pallas kernels: 347 us -> 319 us
  starting transfers between devices: 0 us -> 7.79 us
    pallas_call x1, Pallas kernels: 198 us -> 147 us  [run_block(): pl.pallas_call(block_kernel, out_shape=(jax.ShapeDtypeStruct((R, T, D), B...]
    pallas_call x1, Pallas kernels: 74.6 us -> 91.5 us  [reduce_blocks(): pl.pallas_call(reduce_kernel, out_shape=(jax.ShapeDtypeStruct((ra, ca), F...]
    ppermute x0 -> x5, starting transfers between devices: none -> 7.79 us  [the longest x1 1.69 us: on_device(): outputs = lax.ppermute(outputs, axes, back)]
    pallas_call x1, Pallas kernels: 74.6 us -> 80.3 us  [gather_blocks(): pl.pallas_call(gather_kernel, out_shape=(jax.ShapeDtypeStruct((count,) +...]
  transfers between devices with their start and end apart: 0 -> 5, of which waited for: 0 -> 0; matrix products, arithmetic and copies ran while one was open for 0% -> 4% of each run, Pallas kernels for 0% -> 50%
where the time goes in v3:
time: 346 us; the launch traced here: 345 us
  Pallas kernels  319 us (92%)
  local copies, waits for them, and re-layouts  16.3 us (5%)
  starting transfers between devices  7.79 us (2%)
    pallas_call x1, Pallas kernels, run_block(): pl.pallas_call(block_kernel, out_shape=(jax.ShapeDtypeStruct((R, T, D), B...  147 us
    pallas_call x1, Pallas kernels, reduce_blocks(): pl.pallas_call(reduce_kernel, out_shape=(jax.ShapeDtypeStruct((ra, ca), F...  91.5 us
    pallas_call x1, Pallas kernels, gather_blocks(): pl.pallas_call(gather_kernel, out_shape=(jax.ShapeDtypeStruct((count,) +...  80.3 us
  transfers between devices with their start and end apart: 5, of which 0 were waited for; matrix products, arithmetic and copies ran while one was open for 4% of the time, Pallas kernels for 50%

profile of v3, /device:TPU:0, one launch (start us, length us, event | category | flops | bytes accessed | tf_op | source)
XLA Modules:
  0.0 345.3 jit_solution(3405583068739445806)
XLA Ops:
  0.6 1.3 collective-permute-start.2
  2.0 1.5 collective-permute-start
  3.5 1.7 collective-permute-start.1
  5.2 0.7 copy.30
  5.9 0.7 copy.31
  6.7 0.7 copy.32
  7.4 0.7 copy.33
  8.2 0.8 copy.29
  8.9 0.1 concatenate.6
  9.0 1.7 fusion.1.a_ref
  10.8 80.3 %shard_map.203 = (bf16[32,24,6272]{2,1,0:T(8,128)(2,1)}, bf16[32,96,768]{2,1,0:T(8,128)(2,1)}) custom-call(bf16[24,6272]{1,0:T(8,128)(2,1)} %fusion.1.a_ref, bf16[96,768]{1,0:T(8,128)(2,1)} %b_ref.1), custom_call_target="tpu_custom_call" | custom-call | tf_op jit(solution)/shard_map/pallas_call | solution.py:121
  91.1 0.0 collective-permute-done.2
  91.1 0.1 pad_bitcast_fusion.2
  91.2 0.0 collective-permute-done.1
  91.2 0.2 reshape.42
  91.4 0.9 copy.38
  92.3 0.0 collective-permute-done
  92.3 0.0 copy-start
  92.3 0.6 broadcast_in_dim.11.ids_ref
  92.9 0.0 copy-done
  92.9 147.0 %shard_map.204 = (bf16[5,64,768]{2,1,0:T(8,128)(2,1)}, f32[64,768]{1,0:T(8,128)}, bf16[768,6272]{1,0:T(8,128)(2,1)}, bf16[3072,768]{1,0:T(8,128)(2,1)}) custom-call(bf16[768,6272]{1,0:T(8,128)(2,1)} %bitcast.26, bf16[3072,768]{1,0:T(8,128)(2,1)} %bitcast.28, bf16[64,768]{1,0:T(8,128)(2,1)} %bitcast.32, bf16[5,64,768]{2,1,0:T(8,128)(2,1)} %bitcast.29, ...), custom_call_target="tpu_custom_call" | custom-call | tf_op jit(solution)/shard_map/pallas_call | solution.py:617
  239.9 1.7 collective-permute-start.3
  241.6 1.6 collective-permute-start.4
  243.2 91.5 %shard_map.205 = (f32[24,6272]{1,0:T(8,128)}, f32[96,768]{1,0:T(8,128)}) custom-call(bf16[32,24,6272]{2,1,0:T(8,128)(2,1)} %bitcast.25, bf16[32,96,768]{2,1,0:T(8,128)(2,1)} %bitcast.27), custom_call_target="tpu_custom_call" | custom-call | tf_op jit(solution)/shard_map/pallas_call | solution.py:243
  334.6 0.7 slice_bitcast_fusion
  335.4 1.5 slice.28
  336.9 1.6 slice.27
  338.5 1.7 slice.29
  340.2 0.1 slice.40
  340.3 0.7 copy.36
  341.0 0.7 slice_reduce_fusion
  341.7 0.0 collective-permute-done.4
  341.7 0.0 collective-permute-done.3
  341.7 0.3 copy.35
  342.0 1.0 reshape.43
  343.0 0.7 copy.41
  343.7 1.7 copy.42
  (2 shorter events, 0.0 us)
Async XLA Ops:
  0.6 90.4 %collective-permute-start.2 = (s32[1,64]{1,0:T(1,128)}, s32[1,64]{1,0:T(1,128)S(1)}, u32[]{:S(2)}, u32[]{:S(2)}) collective-permute-start(s32[1,64]{1,0:T(1,128)} %param.22), channel_id=1, source_target_pairs={{0,0},{1,4},{2,1},{3,5},{4,2},{5,6},{6,3},{7,7},{8,8},{9,12},{10,9... | collective-permute-start | bytes 776 | tf_op jit(solution)/shard_map/ppermute | solution.py:679
  2.0 90.3 %collective-permute-start = (bf16[1,64,768]{2,1,0:T(8,128)(2,1)}, bf16[1,64,768]{2,1,0:T(8,128)(2,1)S(1)}, u32[]{:S(2)}, u32[]{:S(2)}) collective-permute-start(bf16[1,64,768]{2,1,0:T(8,128)(2,1)} %param.12), channel_id=1, source_target_pairs={{0,0},{1,4},{2,1},{3,5},{4,2},{5,6},{6,3},{7,7},{8,8},{9,12},{10,9... | collective-permute-start | bytes 294920 | tf_op jit(solution)/shard_map/ppermute | solution.py:680
  3.5 87.7 %collective-permute-start.1 = (bf16[1,320,768]{2,1,0:T(8,128)(2,1)}, bf16[1,320,768]{2,1,0:T(8,128)(2,1)S(1)}, u32[]{:S(2)}, u32[]{:S(2)}) collective-permute-start(bf16[1,320,768]{2,1,0:T(8,128)(2,1)} %param.23), channel_id=1, source_target_pairs={{0,0},{1,4},{2,1},{3,5},{4,2},{5,6},{6,3},{7,7},{8,8},{9,12},{10,9... | collective-permute-start | bytes 1474568 | tf_op jit(solution)/shard_map/ppermute | solution.py:681
  92.3 0.6 copy-start
  239.9 101.8 %collective-permute-start.3 = (bf16[5,64,768]{2,1,0:T(8,128)(2,1)}, bf16[5,64,768]{2,1,0:T(8,128)(2,1)S(1)}, u32[]{:S(2)}, u32[]{:S(2)}) collective-permute-start(bf16[5,64,768]{2,1,0:T(8,128)(2,1)} %get-tuple-element.21), channel_id=1, source_target_pairs={{0,0},{4,1},{1,2},{5,3},{2,4},{6,5},{3,6},{7,7},{8,8},{12,9},{9,10... | collective-permute-start | bytes 1474568 | tf_op jit(solution)/shard_map/ppermute | solution.py:694
  241.6 100.1 %collective-permute-start.4 = (f32[64,768]{1,0:T(8,128)}, f32[64,768]{1,0:T(8,128)S(1)}, u32[]{:S(2)}, u32[]{:S(2)}) collective-permute-start(f32[64,768]{1,0:T(8,128)} %get-tuple-element.22), channel_id=1, source_target_pairs={{0,0},{4,1},{1,2},{5,3},{2,4},{6,5},{3,6},{7,7},{8,8},{12,9},{9,10... | collective-permute-start | bytes 589832 | tf_op jit(solution)/shard_map/ppermute | solution.py:695
